TPU v7x, 1024 devices: a whole 8x8x8 slice. The times are simulated.
1024 devices in a mesh: fsdp: 16 (over x, core), ep: 64 (over z, y).
Axes of the slice: x: 8, y: 8, z: 8, core: 2. Of those that a mesh axis runs over, the one named last changes fastest.
Arguments:
- tokens: bfloat16 [8192, 2048], P(('fsdp', 'ep')), may hold values from -6 to 6
- cotangent: bfloat16 [8192, 2048], P(('fsdp', 'ep')), may hold values from -4 to 4
- routes: int32 [8192, 2], P(('fsdp', 'ep')), may hold values from 0 to 7, as said below
- logits: float32 [8192, 8], P(('fsdp', 'ep')), may hold values from -8 to 8
- w_gate: bfloat16 [2048, 16384], P('fsdp', 'ep'), may hold values from -0.125 to 0.125
- w_up: bfloat16 [2048, 16384], P('fsdp', 'ep'), may hold values from -0.125 to 0.125
- w_down: bfloat16 [16384, 2048], P('ep', 'fsdp'), may hold values from -0.0625 to 0.0625
Outputs:
- grad_tokens: bfloat16 [8192, 2048], P(('fsdp', 'ep'))
- route_dot: float32 [8192, 2], P(('fsdp', 'ep'))
- aux_grad: float32 [8192, 8], P(('fsdp', 'ep'))
- grad_gate: bfloat16 [2048, 16384], P('fsdp', 'ep')
- grad_up: bfloat16 [2048, 16384], P('fsdp', 'ep')
- grad_down: bfloat16 [16384, 2048], P('ep', 'fsdp')
Inputs may be any that keep to these rules, and one draw needn't show every extreme that they name: `routes`: each token names two different experts; on every device at most 3 tokens name one expert, and some expert is named by exactly 3 of them.
All inputs are finite; a program needn't handle non-finite values.
Results may differ from a plain program's by a relative error of at most 0.04.
Values may be sent and summed in bfloat16 or wider, within the bound.
No kernel may reach another device: no remote copies, remote signals or barrier semaphores. Data moves between devices by JAX's collectives and lax.ppermute only.
A program may use at most 32 MiB of HBM per device.

v0:
```python
import jax
import jax.numpy as jnp
from jax import lax
from jax.experimental import pallas as pl
from jax.experimental.pallas import tpu as pltpu
from jax.sharding import Mesh
from jax.sharding import PartitionSpec as P


NX, NC, NZ, NY = 8, 2, 8, 8
ALL = ("x", "c", "z", "y")
SWAP = ((0, 1), (1, 0))
CAP = 3
DM = 2048
HID = 256
BLK = 128
NSRC = NZ * NY
WIRE = 1536
BACK = 896
SHARD = 3 * BLK + 8
ROWS = NSRC * CAP
VM = pl.BlockSpec(memory_space=pltpu.VMEM)
FAR = pl.BlockSpec(memory_space=pltpu.HBM)
bf16, f32, i32 = jnp.bfloat16, jnp.float32, jnp.int32
FIRST = (((0,), (0,)), ((), ()))
LAST = (((1,), (1,)), ((), ()))


def dot(a, b, dims=(((1,), (0,)), ((), ()))):
    return lax.dot_general(a, b, dims, preferred_element_type=f32)


def call(kernel, outs, n_in, limit=16, far=(), scratch=()):
    specs = [FAR if k in far else VM for k in range(n_in)]
    return pl.pallas_call(
        kernel,
        out_shape=outs,
        in_specs=specs,
        out_specs=jax.tree.map(lambda _: VM, outs),
        scratch_shapes=scratch,
        compiler_params=pltpu.CompilerParams(vmem_limit_bytes=limit << 20),
    )


def shape(*dims, dtype=bf16):
    return jax.ShapeDtypeStruct(dims, dtype)


def iota(dims, axis):
    return lax.broadcasted_iota(i32, dims, axis)


def column(row):
    same = iota((8, 8), 0) == iota((8, 8), 1)
    return jnp.sum(jnp.where(same, row.astype(f32), 0.0), axis=1, keepdims=True)


def line(col):
    same = iota((8, 8), 0) == iota((8, 8), 1)
    return jnp.sum(jnp.where(same, col, 0.0), axis=0, keepdims=True)


def slots(routes_t):
    lane = iota((8, 8), 1).astype(f32)
    routes = (column(routes_t[0:1]), column(routes_t[1:2]))
    pick0 = (routes[0] == lane).astype(f32)
    pick1 = (routes[1] == lane).astype(f32)
    member = pick0 + pick1
    below = (iota((8, 8), 1) < iota((8, 8), 0)).astype(f32)
    slot = dot(below, member)
    return pick0, pick1, member, slot


def own_first(v, core):
    even = [v[:, 256 * k : 256 * k + 128] for k in range(8)]
    odd = [v[:, 256 * k + 128 : 256 * k + 256] for k in range(8)]
    mine = [jnp.where(core == 0, a, b) for a, b in zip(even, odd)]
    rest = [jnp.where(core == 0, b, a) for a, b in zip(even, odd)]
    return jnp.concatenate(mine + rest, axis=1)


def in_order(v, core):
    mine = [v[:, 128 * k : 128 * k + 128] for k in range(8)]
    rest = [v[:, 1024 + 128 * k : 1152 + 128 * k] for k in range(8)]
    both = []
    for a, b in zip(mine, rest):
        both += [jnp.where(core == 0, a, b), jnp.where(core == 0, b, a)]
    return jnp.concatenate(both, axis=1)


def pack_weights(routes, w_gate, w_up, w_down, out):
    out[0:BLK] = w_gate[...]
    out[BLK : 2 * BLK] = w_up[...]
    out[2 * BLK : 3 * BLK] = jnp.transpose(w_down[...].astype(f32)).astype(bf16)
    lane = iota((8, HID), 1)
    lane = jnp.where(lane < 16, lane & 7, 8).astype(f32)
    hits = (column(routes[0:1]) == lane).astype(f32) + (column(routes[1:2]) == lane).astype(f32)
    total = jnp.sum(hits, axis=0, keepdims=True)
    row = iota((8, HID), 0)
    out[3 * BLK : SHARD] = jnp.where(row == 0, total, 0.0).astype(bf16)


def send_rows(tokens, cotangent, routes, logits, out):
    core = lax.axis_index("c")
    pick0, pick1, member, slot = slots(routes[...])
    lg = logits[...]
    l0 = jnp.sum(pick0 * lg, axis=1, keepdims=True)
    l1 = jnp.sum(pick1 * lg, axis=1, keepdims=True)
    top = jnp.maximum(l0, l1)
    e0, e1 = jnp.exp(l0 - top), jnp.exp(l1 - top)
    both = e0 + e1
    scaled = pick0 * (e0 / both) + pick1 * (e1 / both)
    tok = own_first(tokens[...].astype(f32), core)
    cot = own_first(cotangent[...].astype(f32), core)
    lane = iota((8, 8), 1)
    tok_b = tok.astype(bf16)
    for x in range(2):
        mem, at = member[:, x : x + 1], slot[:, x : x + 1].astype(i32)
        sel_x = jnp.where((at == lane) & (lane < CAP), mem, 0.0).astype(bf16)
        sel_g = jnp.where((at + CAP == lane) & (lane < 2 * CAP), mem, 0.0).astype(bf16)
        grads = (cot * scaled[:, x : x + 1]).astype(bf16)
        rows = dot(sel_x, tok_b, FIRST) + dot(sel_g, grads, FIRST)
        tail = rows[:, WIRE:].astype(bf16)
        pieces = []
        for r in range(CAP):
            to, fr = iota((8, 8), 0), iota((8, 8), 1)
            move = ((to == 6) & (fr == r)) | ((to == 7) & (fr == CAP + r))
            moved = dot(move.astype(f32).astype(bf16), tail)
            pieces.append((rows[:, 512 * r : 512 * r + 512] + moved).astype(bf16))
        block = jnp.concatenate(pieces, axis=1)
        out[32 * x : 32 * x + 32] = jnp.broadcast_to(block[None], (32, 8, WIRE))


def stack_shards(*refs):
    out, chip = refs[8], lax.axis_index("x")
    for k in range(8):
        out[lax.rem(chip + 8 - k, 8)] = refs[k][...]


def one_hot(cond):
    return cond.astype(f32).astype(bf16)


def weight(ref, k):
    return ref[:, k * BLK : (k + 1) * BLK, :].reshape(DM // 2, HID)


def forward(wire, own, far, x_out, g_out, grads_out, dots_out, oth, sem):
    fetch = pltpu.make_async_copy(far, oth, sem)
    fetch.start()
    to, fr = iota((192, 256), 0), iota((192, 256), 1)
    main = one_hot(fr == 8 * (to & 31) + (to >> 5))
    to, fr = iota((64, 256), 0), iota((64, 256), 1)
    ends = one_hot(fr == 8 * (to & 31) + 6 + (to >> 5))
    for j in range(2):
        part = dot(main, wire[256 * j : 256 * j + 256, :]).astype(bf16)
        x_out[96 * j : 96 * j + 96, 0:WIRE] = part[0:96]
        g_out[96 * j : 96 * j + 96, 0:WIRE] = part[96:192]
        for r in range(CAP):
            at = 96 * j + 32 * r
            tail = dot(ends, wire[256 * j : 256 * j + 256, 512 * r : 512 * r + 512]).astype(bf16)
            x_out[at : at + 32, WIRE:DM] = tail[0:32]
            g_out[at : at + 32, WIRE:DM] = tail[32:64]
    half = DM // 2
    near = [dot(rows[:, 0:half], weight(own, k)) for k, rows in enumerate((x_out, x_out, g_out))]
    fetch.wait()
    gate_pre, up_pre, hidden_grad = [
        near[k] + dot(rows[:, half:DM], weight(oth, k))
        for k, rows in enumerate((x_out, x_out, g_out))
    ]
    sigma = 1.0 / (1.0 + jnp.exp(-gate_pre))
    active = gate_pre * sigma
    hidden = (active * up_pre).astype(bf16)
    part_dot = jnp.sum(hidden.astype(f32) * hidden_grad, axis=1, keepdims=True)
    up_grad = (hidden_grad * active).astype(bf16)
    gate_grad = (hidden_grad * up_pre * sigma * (1.0 + gate_pre * (1.0 - sigma))).astype(bf16)
    grads_out[:, 0:HID] = gate_grad
    grads_out[:, HID : 2 * HID] = up_grad
    grads_out[:, 2 * HID : 3 * HID] = hidden
    lane = iota((ROWS, BLK), 1)
    dots_out[...] = jnp.where(lane == 0, part_dot, 0.0).astype(bf16)


def row_grads(grads, dots, own, oth, back):
    gate_grad, up_grad = grads[:, 0:HID], grads[:, HID : 2 * HID]
    counts = jnp.zeros((8, HID), f32)
    for k in range(8):
        counts = counts + own[k, 3 * BLK : SHARD, :].astype(f32)
        counts = counts + oth[k, 3 * BLK : SHARD, :].astype(f32)
    tally = jnp.sum(counts, axis=0, keepdims=True)[:, 0:BLK]
    px = []
    for ref in (own, oth):
        v = dot(gate_grad, weight(ref, 0), LAST) + dot(up_grad, weight(ref, 1), LAST)
        px.append(v.astype(bf16))
    to, fr = iota((256, 96), 0), iota((256, 96), 1)
    row, slot_of = to & 7, fr >> 5
    same = 8 * ((to >> 3) & 3) + (to >> 5) == (fr & 31)
    first = one_hot(same & (row == 2 * slot_of))
    second = one_hot(same & (row == 2 * slot_of + 1))
    c60 = one_hot(same & (row == 6) & (slot_of == 0))
    c61 = one_hot(same & (row == 6) & (slot_of == 1))
    c71 = one_hot(same & (row == 7) & (slot_of == 1))
    c72 = one_hot(same & (row == 7) & (slot_of == 2))
    for_dot = one_hot(same & (row == slot_of))
    count_at = (iota((256, BLK), 0) & 7) == CAP
    for j in range(2):

        def piece(k):
            v = px[k // 4]
            k = k % 4
            return v[96 * j : 96 * j + 96, 256 * k : 256 * k + 256]

        def store(v, lo, hi):
            for y in range(8):
                at = 64 * y + 32 * j
                back[at : at + 32, lo:hi] = v[32 * y : 32 * y + 32]

        lo, hi = piece(6), piece(7)
        ends = ((c60, lo, c71, hi), (c60, hi, c72, lo), (c61, lo, c72, hi))
        for n in range(3):
            a, va, b, vb = ends[n]
            v = dot(first, piece(n)) + dot(second, piece(n + 3)) + dot(a, va) + dot(b, vb)
            store(v.astype(bf16), 256 * n, 256 * n + 256)
        last = dot(for_dot, dots[96 * j : 96 * j + 96, :]) + jnp.where(count_at, tally, 0.0)
        store(last.astype(bf16), 768, BACK)


def sum_y(came, out):
    s = came[0:64, :].astype(f32)
    for k in range(1, 8):
        s = s + came[64 * k : 64 * k + 64, :].astype(f32)
    out[:, 0:768] = s[:, 0:768].astype(bf16)
    last = s[:, 768:BACK]
    high = jnp.floor(last * 0.0625)
    digit = jnp.where(iota((64, BLK), 1) < 8, last - 16.0 * high, high)
    out[:, 768:BACK] = jnp.where((iota((64, BLK), 0) & 7) == CAP, digit, last).astype(bf16)


def weight_grads(x_rows, g_rows, grads, keep, send):
    half = DM // 2
    for ref, at in ((send, half), (keep, 0)):
        for k, rows in ((0, x_rows), (1, x_rows), (2, g_rows)):
            v = dot(rows[:, at : at + half], grads[:, k * HID : (k + 1) * HID], FIRST)
            ref[:, k * BLK : (k + 1) * BLK, :] = v.astype(bf16).reshape(8, BLK, HID)


def add_cores(keep, came, *outs):
    chip = lax.axis_index("x")
    for k in range(8):
        at = lax.rem(chip + k, 8)
        outs[k][...] = (keep[at].astype(f32) + came[at].astype(f32)).astype(bf16)


def join(*refs):
    s2, a, d, s6, b, t2, t6 = refs
    t2[...] = (s2[...].astype(f32) + a[...].astype(f32) + d[...].astype(f32)).astype(bf16)
    t6[...] = (s6[...].astype(f32) + b[...].astype(f32)).astype(bf16)


def sum_chips(*refs):
    ins, (gate, up, down) = refs[:5], refs[5:]
    for k, ref in ((0, gate), (1, up), (2, down)):
        total = ins[0][k * BLK : (k + 1) * BLK].astype(f32)
        for i in range(1, 5):
            total = total + ins[i][k * BLK : (k + 1) * BLK].astype(f32)
        ref[...] = (jnp.transpose(total) if k == 2 else total).astype(bf16)


def finish(back, routes, logits, grad_tokens, route_dot, aux_grad):
    core = lax.axis_index("c")
    _, _, member, slot = slots(routes[...])
    total = jnp.zeros((8, DM), f32)
    counts = jnp.zeros((1, BLK), f32)
    dots = []
    for x in range(2):
        s = jnp.zeros((8, BACK), f32)
        for n in range(4):
            at = 8 * (4 * x + n)
            s = s + back[at : at + 8, :].astype(f32)
        counts = counts + s[CAP : CAP + 1, 768:BACK]
        at = slot[:, x : x + 1].astype(i32)
        ends = (
            s[6:7, 0:512],
            jnp.concatenate([s[6:7, 512:768], s[7:8, 0:256]], axis=1),
            s[7:8, 256:768],
        )
        dot_x = jnp.zeros((8, 1), f32)
        for r in range(CAP):
            sel = jnp.where(at == r, member[:, x : x + 1], 0.0)
            row = jnp.concatenate(
                [s[2 * r : 2 * r + 1, 0:768], s[2 * r + 1 : 2 * r + 2, 0:768], ends[r]], axis=1
            )
            total = total + sel * row
            dot_x = dot_x + sel * s[r : r + 1, 768:769]
        dots.append(dot_x)
    grad_tokens[...] = in_order(total, core).astype(bf16)
    row2 = iota((2, 8), 0)
    route_dot[...] = jnp.where(row2 == 0, line(dots[0]), line(dots[1]))
    lg = logits[...]
    e = jnp.exp(lg - jnp.max(lg, axis=1, keepdims=True))
    probs = e / jnp.sum(e, axis=1, keepdims=True)
    cnt = counts[:, 0:8] + 16.0 * counts[:, 8:16]
    target = 8.0 * (cnt / jnp.sum(cnt, axis=1, keepdims=True))
    aux_grad[...] = probs * (target - jnp.sum(probs * target, axis=1, keepdims=True))


def shifted(value, by):
    return lax.ppermute(value, "x", [(i, (i + by) % NX) for i in range(NX)])


def exchange(value, axis):
    return lax.all_to_all(value, axis, split_axis=0, concat_axis=0, tiled=True)


def body(tokens, cotangent, routes, logits, w_gate, w_up, w_down):
    routes_t = routes.T
    shard = call(pack_weights, shape(SHARD, HID), 4, limit=60)(routes_t, w_gate, w_up, w_down)
    p2 = shifted(shard, 2)
    m2 = shifted(shard, 6)
    wire = call(send_rows, shape(NSRC, 8, WIRE), 4, limit=60)(tokens, cotangent, routes_t, logits)
    came = exchange(wire, ("z", "y"))
    p1 = shifted(shard, 1)
    m1 = shifted(shard, 7)
    p4 = shifted(p2, 2)
    p3 = shifted(p2, 1)
    m3 = shifted(m2, 7)
    own = call(stack_shards, shape(8, SHARD, HID), 8)(shard, p1, p2, p3, p4, m3, m2, m1)
    oth = lax.ppermute(own, "c", SWAP)
    x_rows, g_rows, grads, dots, oth = call(
        forward,
        (
            shape(ROWS, DM),
            shape(ROWS, DM),
            shape(ROWS, 3 * HID),
            shape(ROWS, BLK),
            shape(8, SHARD, HID),
        ),
        3,
        far=(2,),
        scratch=(pltpu.SemaphoreType.DMA,),
    )(came.reshape(8 * NSRC, WIRE), own, oth)
    keep, send = call(
        weight_grads, (shape(8, 3 * BLK, HID), shape(8, 3 * BLK, HID)), 3
    )(x_rows, g_rows, grads)
    other = lax.ppermute(send, "c", SWAP)
    back = call(row_grads, shape(8 * NSRC, BACK), 4)(grads, dots, own, oth)
    back = exchange(back.reshape(NY, 8 * NZ, BACK), "y")
    s = call(add_cores, tuple(shape(3 * BLK, HID) for _ in range(8)), 2)(keep, other)
    a, d, b = shifted(s[3], 1), shifted(s[4], 2), shifted(s[5], 7)
    e1 = shifted(s[1], 1)
    e7 = shifted(s[7], 7)
    t2, t6 = call(join, (shape(3 * BLK, HID), shape(3 * BLK, HID)), 5)(s[2], a, d, s[6], b)
    e2, e6 = shifted(t2, 2), shifted(t6, 6)
    back = call(sum_y, shape(8 * NZ, BACK), 1)(back.reshape(8 * NSRC, BACK))
    back = exchange(back.reshape(NZ, 8, BACK), "z")
    grad_gate, grad_up, grad_down = call(
        sum_chips, (shape(BLK, HID), shape(BLK, HID), shape(HID, BLK)), 5
    )(s[0], e1, e7, e2, e6)
    grad_tokens, route_dot, aux_grad = call(
        finish, (shape(8, DM), shape(2, 8, dtype=f32), shape(8, 8, dtype=f32)), 3
    )(back.reshape(8 * NZ, BACK), routes_t, logits)
    return (grad_tokens, route_dot.T, aux_grad, grad_gate, grad_up, grad_down)


def solution(mesh):
    split = Mesh(mesh.devices.reshape(NX, NC, NZ, NY), ALL)
    rows, cols, down = P(ALL, None), P(("x", "c"), ("z", "y")), P(("z", "y"), ("x", "c"))

    return jax.shard_map(
        body,
        mesh=split,
        in_specs=(rows, rows, rows, rows, cols, cols, down),
        out_specs=(rows, rows, rows, cols, cols, down),
        check_vma=False,
    )
```

profile of v0, /device:TPU:1, one launch (start us, length us, event | category | flops | bytes accessed | tf_op | source)
XLA Modules:
  0.0 148.8 jit_solution(16762294157369323497)
XLA Ops:
  0.6 2.8 %shard_map.118 = bf16[64,8,1536]{2,1,0:T(8,128)(2,1)} custom-call(bf16[8,2048]{1,0:T(8,128)(2,1)} %tokens.1, bf16[8,2048]{1,0:T(8,128)(2,1)} %cotangent.1, s32[2,8]{1,0:T(2,128)} %bitcast.10, f32[8,8]{1,0:T(8,128)} %logits.3), custom_call_target="tpu_custom_call" | custom-call | tf_op jit(solution)/shard_map/pallas_call | solution.py:320
  3.4 23.9 %all-to-all-start = ((bf16[64,8,1536]{2,1,0:T(8,128)(2,1)}), bf16[64,8,1536]{2,1,0:T(8,128)(2,1)S(1)}, u32[]{:S(2)}, u32[]{:S(2)}) async-start(bf16[64,8,1536]{2,1,0:T(8,128)(2,1)} %shard_map.118), calls=%async_computation | async-start | bytes 3145728 | tf_op jit(solution)/shard_map/all_to_all | solution.py:312
  27.4 1.7 %shard_map.119.refs_0_ = bf16[392,256]{1,0:T(8,128)(2,1)} custom-call(s32[2,8]{1,0:T(2,128)} %bitcast.11, bf16[128,256]{1,0:T(8,128)(2,1)} %w_gate.1, bf16[128,256]{1,0:T(8,128)(2,1)} %w_up.1, bf16[256,128]{1,0:T(8,128)(2,1)} %w_down.1), custom_call_target="tpu_custom_call" | custom-call | tf_op jit(solution)/shard_map/pallas_call | solution.py:317
  29.1 5.4 %collective-permute-start.4 = (bf16[392,256]{1,0:T(8,128)(2,1)}, bf16[392,256]{1,0:T(8,128)(2,1)S(1)}, u32[]{:S(2)}, u32[]{:S(2)}) collective-permute-start(bf16[392,256]{1,0:T(8,128)(2,1)} %shard_map.119.refs_0_), channel_id=1, source_target_pairs={{0,768},{128,896},{256,0},{384,128},{512,256},{640,384},{768,512},... | collective-permute-start | bytes 602120 | tf_op jit(solution)/shard_map/ppermute | solution.py:308
  34.4 1.9 %collective-permute-start.1 = (bf16[392,256]{1,0:T(8,128)(2,1)}, bf16[392,256]{1,0:T(8,128)(2,1)S(1)}, u32[]{:S(2)}, u32[]{:S(2)}) collective-permute-start(bf16[392,256]{1,0:T(8,128)(2,1)} %shard_map.119.refs_0_), channel_id=1, source_target_pairs={{0,256},{128,384},{256,512},{384,640},{512,768},{640,896},{768,0},... | collective-permute-start | bytes 602120 | tf_op jit(solution)/shard_map/ppermute | solution.py:308
  36.4 4.6 %collective-permute-start.6 = (bf16[392,256]{1,0:T(8,128)(2,1)}, bf16[392,256]{1,0:T(8,128)(2,1)S(1)}, u32[]{:S(2)}, u32[]{:S(2)}) collective-permute-start(bf16[392,256]{1,0:T(8,128)(2,1)} %shard_map.119.refs_0_), channel_id=1, source_target_pairs={{0,896},{128,0},{256,128},{384,256},{512,384},{640,512},{768,640},... | collective-permute-start | bytes 602120 | tf_op jit(solution)/shard_map/ppermute | solution.py:308
  41.0 1.9 %collective-permute-start = (bf16[392,256]{1,0:T(8,128)(2,1)}, bf16[392,256]{1,0:T(8,128)(2,1)S(1)}, u32[]{:S(2)}, u32[]{:S(2)}) collective-permute-start(bf16[392,256]{1,0:T(8,128)(2,1)} %shard_map.119.refs_0_), channel_id=1, source_target_pairs={{0,128},{128,256},{256,384},{384,512},{512,640},{640,768},{768,896... | collective-permute-start | bytes 602120 | tf_op jit(solution)/shard_map/ppermute | solution.py:308
  43.6 3.9 %collective-permute-start.5 = (bf16[392,256]{1,0:T(8,128)(2,1)S(1)}, bf16[392,256]{1,0:T(8,128)(2,1)S(1)}, u32[]{:S(2)}, u32[]{:S(2)}) collective-permute-start(bf16[392,256]{1,0:T(8,128)(2,1)S(1)} %collective-permute-done.4.refs_6_), channel_id=1, source_target_pairs={{0,896},{128,0},{256,128},{384,256},{512,384},{640,512},{768,640},... | collective-permute-start | bytes 602120 | tf_op jit(solution)/shard_map/ppermute | solution.py:308
  47.5 2.0 %collective-permute-start.3 = (bf16[392,256]{1,0:T(8,128)(2,1)S(1)}, bf16[392,256]{1,0:T(8,128)(2,1)S(1)}, u32[]{:S(2)}, u32[]{:S(2)}) collective-permute-start(bf16[392,256]{1,0:T(8,128)(2,1)S(1)} %collective-permute-done.1.refs_2_), channel_id=1, source_target_pairs={{0,256},{128,384},{256,512},{384,640},{512,768},{640,896},{768,0},... | collective-permute-start | bytes 602120 | tf_op jit(solution)/shard_map/ppermute | solution.py:308
  49.5 3.4 %collective-permute-start.2 = (bf16[392,256]{1,0:T(8,128)(2,1)S(1)}, bf16[392,256]{1,0:T(8,128)(2,1)S(1)}, u32[]{:S(2)}, u32[]{:S(2)}) collective-permute-start(bf16[392,256]{1,0:T(8,128)(2,1)S(1)} %collective-permute-done.1.refs_2_), channel_id=1, source_target_pairs={{0,128},{128,256},{256,384},{384,512},{512,640},{640,768},{768,896... | collective-permute-start | bytes 602120 | tf_op jit(solution)/shard_map/ppermute | solution.py:308
  52.9 3.6 %collective-permute-done.3.refs_4_ = bf16[392,256]{1,0:T(8,128)(2,1)S(1)} collective-permute-done((bf16[392,256]{1,0:T(8,128)(2,1)S(1)}, bf16[392,256]{1,0:T(8,128)(2,1)S(1)}, u32[]{:S(2)}, u32[]{:S(2)}) %collective-permute-start.3) | collective-permute-done | bytes 200736 | tf_op jit(solution)/shard_map/ppermute | solution.py:308
  56.5 6.4 %collective-permute-done.2.refs_3_ = bf16[392,256]{1,0:T(8,128)(2,1)S(1)} collective-permute-done((bf16[392,256]{1,0:T(8,128)(2,1)S(1)}, bf16[392,256]{1,0:T(8,128)(2,1)S(1)}, u32[]{:S(2)}, u32[]{:S(2)}) %collective-permute-start.2) | collective-permute-done | bytes 200736 | tf_op jit(solution)/shard_map/ppermute | solution.py:308
  63.9 5.9 %collective-permute-start.7 = (bf16[8,392,256]{2,1,0:T(8,128)(2,1)S(1)}, bf16[8,392,256]{2,1,0:T(8,128)(2,1)S(1)}, u32[]{:S(2)}, u32[]{:S(2)}) collective-permute-start(bf16[8,392,256]{2,1,0:T(8,128)(2,1)S(1)} %shard_map.120.own), channel_id=1, source_target_pairs={{0,64},{64,0},{1,65},{65,1},{2,66},{66,2},{3,67},{67,3},{4,68},{68... | collective-permute-start | bytes 4816904 | tf_op jit(solution)/shard_map/ppermute | solution.py:328
  69.8 3.1 %collective-permute-done.7.far = bf16[8,392,256]{2,1,0:T(8,128)(2,1)S(1)} collective-permute-done((bf16[8,392,256]{2,1,0:T(8,128)(2,1)S(1)}, bf16[8,392,256]{2,1,0:T(8,128)(2,1)S(1)}, u32[]{:S(2)}, u32[]{:S(2)}) %collective-permute-start.7) | collective-permute-done | bytes 1605664 | tf_op jit(solution)/shard_map/ppermute | solution.py:328
  74.0 1.4 copy-done.1
  75.4 2.1 %shard_map.121 = (bf16[192,2048]{1,0:T(8,128)(2,1)S(1)}, bf16[192,2048]{1,0:T(8,128)(2,1)S(1)}, bf16[192,768]{1,0:T(8,128)(2,1)S(1)}, bf16[192,128]{1,0:T(8,128)(2,1)S(1)}, bf16[8,392,256]{2,1,0:T(8,128)(2,1)S(1)}) custom-call(bf16[512,1536]{1,0:T(8,128)(2,1)S(1)} %bitcast.7, bf16[8,392,256]{2,1,0:T(8,128)(2,1)S(1)} %shard_map.120.own, ...), custom_call_target="tpu_custom_call" | custom-call | tf_op jit(solution)/shard_map/pallas_call | solution.py:329
  77.6 1.9 %shard_map.125 = (bf16[8,384,256]{2,1,0:T(8,128)(2,1)S(1)}, bf16[8,384,256]{2,1,0:T(8,128)(2,1)}) custom-call(bf16[192,2048]{1,0:T(8,128)(2,1)S(1)} %get-tuple-element.35.x_rows, bf16[192,2048]{1,0:T(8,128)(2,1)S(1)} %get-tuple-element.36.g_rows, bf16[192,768]{1,0:T(8,128)(2,1)S(1)} %get-tuple-element.29.grads), custom_call_target="tpu_custom_call" | custom-call | tf_op jit(solution)/shard_map/pallas_call | solution.py:342
  79.5 2.3 %collective-permute-start.8 = (bf16[8,384,256]{2,1,0:T(8,128)(2,1)}, bf16[8,384,256]{2,1,0:T(8,128)(2,1)}, u32[]{:S(2)}, u32[]{:S(2)}) collective-permute-start(bf16[8,384,256]{2,1,0:T(8,128)(2,1)} %get-tuple-element.38), channel_id=1, source_target_pairs={{0,64},{64,0},{1,65},{65,1},{2,66},{66,2},{3,67},{67,3},{4,68},{68... | collective-permute-start | bytes 4718600 | tf_op jit(solution)/shard_map/ppermute | solution.py:345
  81.8 2.6 %shard_map.122 = bf16[512,896]{1,0:T(8,128)(2,1)} custom-call(bf16[192,768]{1,0:T(8,128)(2,1)S(1)} %get-tuple-element.29.grads, bf16[192,128]{1,0:T(8,128)(2,1)S(1)} %get-tuple-element.30.dots, bf16[8,392,256]{2,1,0:T(8,128)(2,1)S(1)} %shard_map.120.own, bf16[8,392,256]{2,1,0:T(8,128)(2,1)S(1)} %get-tuple-element.31.oth), custom_call_target="tpu_custom_call" | custom-call | tf_op jit(solution)/shard_map/pallas_call | solution.py:346
  84.4 6.2 %all-to-all-start.1 = ((bf16[8,64,896]{2,1,0:T(8,128)(2,1)}), bf16[8,64,896]{2,1,0:T(8,128)(2,1)S(1)}, u32[]{:S(2)}, u32[]{:S(2)}) async-start(bf16[8,64,896]{2,1,0:T(8,128)(2,1)} %bitcast.2), calls=%async_computation.1 | async-start | bytes 1835008 | tf_op jit(solution)/shard_map/all_to_all | solution.py:312
  90.6 2.4 %shard_map.126 = (bf16[384,256]{1,0:T(8,128)(2,1)S(1)}, bf16[384,256]{1,0:T(8,128)(2,1)S(1)}, bf16[384,256]{1,0:T(8,128)(2,1)S(1)}, bf16[384,256]{1,0:T(8,128)(2...) custom-call(bf16[8,384,256]{2,1,0:T(8,128)(2,1)S(1)} %get-tuple-elem, ...), custom_call_target="tpu_custom_call" | custom-call | tf_op jit(solution)/shard_map/pallas_call | solution.py:348
  93.1 2.0 %collective-permute-start.11 = (bf16[384,256]{1,0:T(8,128)(2,1)}, bf16[384,256]{1,0:T(8,128)(2,1)S(1)}, u32[]{:S(2)}, u32[]{:S(2)}) collective-permute-start(bf16[384,256]{1,0:T(8,128)(2,1)} %get-tuple-element.43), channel_id=1, source_target_pairs={{0,128},{128,256},{256,384},{384,512},{512,640},{640,768},{768,896... | collective-permute-start | bytes 589832 | tf_op jit(solution)/shard_map/ppermute | solution.py:308
  95.1 3.3 %collective-permute-start.12 = (bf16[384,256]{1,0:T(8,128)(2,1)}, bf16[384,256]{1,0:T(8,128)(2,1)S(1)}, u32[]{:S(2)}, u32[]{:S(2)}) collective-permute-start(bf16[384,256]{1,0:T(8,128)(2,1)} %get-tuple-element.44), channel_id=1, source_target_pairs={{0,256},{128,384},{256,512},{384,640},{512,768},{640,896},{768,0},... | collective-permute-start | bytes 589832 | tf_op jit(solution)/shard_map/ppermute | solution.py:308
  98.4 3.2 %collective-permute-start.13 = (bf16[384,256]{1,0:T(8,128)(2,1)}, bf16[384,256]{1,0:T(8,128)(2,1)S(1)}, u32[]{:S(2)}, u32[]{:S(2)}) collective-permute-start(bf16[384,256]{1,0:T(8,128)(2,1)} %get-tuple-element.46), channel_id=1, source_target_pairs={{0,896},{128,0},{256,128},{384,256},{512,384},{640,512},{768,640},... | collective-permute-start | bytes 589832 | tf_op jit(solution)/shard_map/ppermute | solution.py:308
  101.6 15.4 %all-to-all-done.1 = bf16[8,64,896]{2,1,0:T(8,128)(2,1)S(1)} async-done(((bf16[8,64,896]{2,1,0:T(8,128)(2,1)}), bf16[8,64,896]{2,1,0:T(8,128)(2,1)S(1)}, u32[]{:S(2)}, u32[]{:S(2)}) %all-to-all-start.1) | async-done | bytes 917536 | tf_op jit(solution)/shard_map/all_to_all | solution.py:312
  117.8 6.5 %all-to-all-start.2 = ((bf16[8,8,896]{2,1,0:T(8,128)(2,1)}), bf16[8,8,896]{2,1,0:T(8,128)(2,1)S(1)}, u32[]{:S(2)}, u32[]{:S(2)}) async-start(bf16[8,8,896]{2,1,0:T(8,128)(2,1)} %bitcast.4), calls=%async_computation.2 | async-start | bytes 229376 | tf_op jit(solution)/shard_map/all_to_all | solution.py:312
  124.3 1.9 %collective-permute-start.9 = (bf16[384,256]{1,0:T(8,128)(2,1)S(1)}, bf16[384,256]{1,0:T(8,128)(2,1)S(1)}, u32[]{:S(2)}, u32[]{:S(2)}) collective-permute-start(bf16[384,256]{1,0:T(8,128)(2,1)S(1)} %get-tuple-element.40), channel_id=1, source_target_pairs={{0,128},{128,256},{256,384},{384,512},{512,640},{640,768},{768,896... | collective-permute-start | bytes 589832 | tf_op jit(solution)/shard_map/ppermute | solution.py:308
  126.2 4.6 %collective-permute-start.10 = (bf16[384,256]{1,0:T(8,128)(2,1)S(1)}, bf16[384,256]{1,0:T(8,128)(2,1)S(1)}, u32[]{:S(2)}, u32[]{:S(2)}) collective-permute-start(bf16[384,256]{1,0:T(8,128)(2,1)S(1)} %get-tuple-element.41), channel_id=1, source_target_pairs={{0,896},{128,0},{256,128},{384,256},{512,384},{640,512},{768,640},... | collective-permute-start | bytes 589832 | tf_op jit(solution)/shard_map/ppermute | solution.py:308
  131.0 1.9 %collective-permute-start.14 = (bf16[384,256]{1,0:T(8,128)(2,1)S(1)}, bf16[384,256]{1,0:T(8,128)(2,1)S(1)}, u32[]{:S(2)}, u32[]{:S(2)}) collective-permute-start(bf16[384,256]{1,0:T(8,128)(2,1)S(1)} %get-tuple-element.47), channel_id=1, source_target_pairs={{0,256},{128,384},{256,512},{384,640},{512,768},{640,896},{768,0},... | collective-permute-start | bytes 589832 | tf_op jit(solution)/shard_map/ppermute | solution.py:308
  132.9 5.5 %collective-permute-start.15 = (bf16[384,256]{1,0:T(8,128)(2,1)S(1)}, bf16[384,256]{1,0:T(8,128)(2,1)S(1)}, u32[]{:S(2)}, u32[]{:S(2)}) collective-permute-start(bf16[384,256]{1,0:T(8,128)(2,1)S(1)} %get-tuple-element.48), channel_id=1, source_target_pairs={{0,768},{128,896},{256,0},{384,128},{512,256},{640,384},{768,512},... | collective-permute-start | bytes 589832 | tf_op jit(solution)/shard_map/ppermute | solution.py:308
  139.4 4.2 %collective-permute-done.14.refs_3_ = bf16[384,256]{1,0:T(8,128)(2,1)S(1)} collective-permute-done((bf16[384,256]{1,0:T(8,128)(2,1)S(1)}, bf16[384,256]{1,0:T(8,128)(2,1)S(1)}, u32[]{:S(2)}, u32[]{:S(2)}) %collective-permute-start.14) | collective-permute-done | bytes 196640 | tf_op jit(solution)/shard_map/ppermute | solution.py:308
  143.5 4.5 %collective-permute-done.15.refs_4_ = bf16[384,256]{1,0:T(8,128)(2,1)S(1)} collective-permute-done((bf16[384,256]{1,0:T(8,128)(2,1)S(1)}, bf16[384,256]{1,0:T(8,128)(2,1)S(1)}, u32[]{:S(2)}, u32[]{:S(2)}) %collective-permute-start.15) | collective-permute-done | bytes 196640 | tf_op jit(solution)/shard_map/ppermute | solution.py:308
  (27 shorter events, 5.6 us)
Async XLA Ops:
  3.4 70.6 %all-to-all-start = ((bf16[64,8,1536]{2,1,0:T(8,128)(2,1)}), bf16[64,8,1536]{2,1,0:T(8,128)(2,1)S(1)}, u32[]{:S(2)}, u32[]{:S(2)}) async-start(bf16[64,8,1536]{2,1,0:T(8,128)(2,1)} %shard_map.118), calls=%async_computation | async-start | bytes 3145728 | tf_op jit(solution)/shard_map/all_to_all | solution.py:312
  29.1 14.5 %collective-permute-start.4 = (bf16[392,256]{1,0:T(8,128)(2,1)}, bf16[392,256]{1,0:T(8,128)(2,1)S(1)}, u32[]{:S(2)}, u32[]{:S(2)}) collective-permute-start(bf16[392,256]{1,0:T(8,128)(2,1)} %shard_map.119.refs_0_), channel_id=1, source_target_pairs={{0,768},{128,896},{256,0},{384,128},{512,256},{640,384},{768,512},... | collective-permute-start | bytes 602120 | tf_op jit(solution)/shard_map/ppermute | solution.py:308
  34.4 13.1 %collective-permute-start.1 = (bf16[392,256]{1,0:T(8,128)(2,1)}, bf16[392,256]{1,0:T(8,128)(2,1)S(1)}, u32[]{:S(2)}, u32[]{:S(2)}) collective-permute-start(bf16[392,256]{1,0:T(8,128)(2,1)} %shard_map.119.refs_0_), channel_id=1, source_target_pairs={{0,256},{128,384},{256,512},{384,640},{512,768},{640,896},{768,0},... | collective-permute-start | bytes 602120 | tf_op jit(solution)/shard_map/ppermute | solution.py:308
  36.4 16.6 %collective-permute-start.6 = (bf16[392,256]{1,0:T(8,128)(2,1)}, bf16[392,256]{1,0:T(8,128)(2,1)S(1)}, u32[]{:S(2)}, u32[]{:S(2)}) collective-permute-start(bf16[392,256]{1,0:T(8,128)(2,1)} %shard_map.119.refs_0_), channel_id=1, source_target_pairs={{0,896},{128,0},{256,128},{384,256},{512,384},{640,512},{768,640},... | collective-permute-start | bytes 602120 | tf_op jit(solution)/shard_map/ppermute | solution.py:308
  41.0 12.0 %collective-permute-start = (bf16[392,256]{1,0:T(8,128)(2,1)}, bf16[392,256]{1,0:T(8,128)(2,1)S(1)}, u32[]{:S(2)}, u32[]{:S(2)}) collective-permute-start(bf16[392,256]{1,0:T(8,128)(2,1)} %shard_map.119.refs_0_), channel_id=1, source_target_pairs={{0,128},{128,256},{256,384},{384,512},{512,640},{640,768},{768,896... | collective-permute-start | bytes 602120 | tf_op jit(solution)/shard_map/ppermute | solution.py:308
  43.6 9.4 %collective-permute-start.5 = (bf16[392,256]{1,0:T(8,128)(2,1)S(1)}, bf16[392,256]{1,0:T(8,128)(2,1)S(1)}, u32[]{:S(2)}, u32[]{:S(2)}) collective-permute-start(bf16[392,256]{1,0:T(8,128)(2,1)S(1)} %collective-permute-done.4.refs_6_), channel_id=1, source_target_pairs={{0,896},{128,0},{256,128},{384,256},{512,384},{640,512},{768,640},... | collective-permute-start | bytes 602120 | tf_op jit(solution)/shard_map/ppermute | solution.py:308
  47.5 9.0 %collective-permute-start.3 = (bf16[392,256]{1,0:T(8,128)(2,1)S(1)}, bf16[392,256]{1,0:T(8,128)(2,1)S(1)}, u32[]{:S(2)}, u32[]{:S(2)}) collective-permute-start(bf16[392,256]{1,0:T(8,128)(2,1)S(1)} %collective-permute-done.1.refs_2_), channel_id=1, source_target_pairs={{0,256},{128,384},{256,512},{384,640},{512,768},{640,896},{768,0},... | collective-permute-start | bytes 602120 | tf_op jit(solution)/shard_map/ppermute | solution.py:308
  49.5 13.3 %collective-permute-start.2 = (bf16[392,256]{1,0:T(8,128)(2,1)S(1)}, bf16[392,256]{1,0:T(8,128)(2,1)S(1)}, u32[]{:S(2)}, u32[]{:S(2)}) collective-permute-start(bf16[392,256]{1,0:T(8,128)(2,1)S(1)} %collective-permute-done.1.refs_2_), channel_id=1, source_target_pairs={{0,128},{128,256},{256,384},{384,512},{512,640},{640,768},{768,896... | collective-permute-start | bytes 602120 | tf_op jit(solution)/shard_map/ppermute | solution.py:308
  62.9 0.9 copy-start.2
  63.9 8.9 %collective-permute-start.7 = (bf16[8,392,256]{2,1,0:T(8,128)(2,1)S(1)}, bf16[8,392,256]{2,1,0:T(8,128)(2,1)S(1)}, u32[]{:S(2)}, u32[]{:S(2)}) collective-permute-start(bf16[8,392,256]{2,1,0:T(8,128)(2,1)S(1)} %shard_map.120.own), channel_id=1, source_target_pairs={{0,64},{64,0},{1,65},{65,1},{2,66},{66,2},{3,67},{67,3},{4,68},{68... | collective-permute-start | bytes 4816904 | tf_op jit(solution)/shard_map/ppermute | solution.py:328
  72.8 1.2 copy-start
  74.0 1.4 copy-start.1
  79.5 11.1 %collective-permute-start.8 = (bf16[8,384,256]{2,1,0:T(8,128)(2,1)}, bf16[8,384,256]{2,1,0:T(8,128)(2,1)}, u32[]{:S(2)}, u32[]{:S(2)}) collective-permute-start(bf16[8,384,256]{2,1,0:T(8,128)(2,1)} %get-tuple-element.38), channel_id=1, source_target_pairs={{0,64},{64,0},{1,65},{65,1},{2,66},{66,2},{3,67},{67,3},{4,68},{68... | collective-permute-start | bytes 4718600 | tf_op jit(solution)/shard_map/ppermute | solution.py:345
  84.4 32.6 %all-to-all-start.1 = ((bf16[8,64,896]{2,1,0:T(8,128)(2,1)}), bf16[8,64,896]{2,1,0:T(8,128)(2,1)S(1)}, u32[]{:S(2)}, u32[]{:S(2)}) async-start(bf16[8,64,896]{2,1,0:T(8,128)(2,1)} %bitcast.2), calls=%async_computation.1 | async-start | bytes 1835008 | tf_op jit(solution)/shard_map/all_to_all | solution.py:312
  93.1 45.3 %copy-start.3 = (f32[8,8]{1,0:T(8,128)S(1)}, f32[8,8]{1,0:T(8,128)}, u32[]{:S(2)}) copy-start(f32[8,8]{1,0:T(8,128)} %logits.3) | copy-start | bytes 772
  93.1 45.3 %copy-start.4 = (s32[8,2]{0,1:T(2,128)S(1)}, s32[8,2]{0,1:T(2,128)}, u32[]{:S(2)}) copy-start(s32[8,2]{0,1:T(2,128)} %param.9) | copy-start | bytes 196
  93.1 37.7 %collective-permute-start.11 = (bf16[384,256]{1,0:T(8,128)(2,1)}, bf16[384,256]{1,0:T(8,128)(2,1)S(1)}, u32[]{:S(2)}, u32[]{:S(2)}) collective-permute-start(bf16[384,256]{1,0:T(8,128)(2,1)} %get-tuple-element.43), channel_id=1, source_target_pairs={{0,128},{128,256},{256,384},{384,512},{512,640},{640,768},{768,896... | collective-permute-start | bytes 589832 | tf_op jit(solution)/shard_map/ppermute | solution.py:308
  95.1 35.7 %collective-permute-start.12 = (bf16[384,256]{1,0:T(8,128)(2,1)}, bf16[384,256]{1,0:T(8,128)(2,1)S(1)}, u32[]{:S(2)}, u32[]{:S(2)}) collective-permute-start(bf16[384,256]{1,0:T(8,128)(2,1)} %get-tuple-element.44), channel_id=1, source_target_pairs={{0,256},{128,384},{256,512},{384,640},{512,768},{640,896},{768,0},... | collective-permute-start | bytes 589832 | tf_op jit(solution)/shard_map/ppermute | solution.py:308
  98.4 32.4 %collective-permute-start.13 = (bf16[384,256]{1,0:T(8,128)(2,1)}, bf16[384,256]{1,0:T(8,128)(2,1)S(1)}, u32[]{:S(2)}, u32[]{:S(2)}) collective-permute-start(bf16[384,256]{1,0:T(8,128)(2,1)} %get-tuple-element.46), channel_id=1, source_target_pairs={{0,896},{128,0},{256,128},{384,256},{512,384},{640,512},{768,640},... | collective-permute-start | bytes 589832 | tf_op jit(solution)/shard_map/ppermute | solution.py:308
  117.8 20.6 %all-to-all-start.2 = ((bf16[8,8,896]{2,1,0:T(8,128)(2,1)}), bf16[8,8,896]{2,1,0:T(8,128)(2,1)S(1)}, u32[]{:S(2)}, u32[]{:S(2)}) async-start(bf16[8,8,896]{2,1,0:T(8,128)(2,1)} %bitcast.4), calls=%async_computation.2 | async-start | bytes 229376 | tf_op jit(solution)/shard_map/all_to_all | solution.py:312
  124.3 15.0 %collective-permute-start.9 = (bf16[384,256]{1,0:T(8,128)(2,1)S(1)}, bf16[384,256]{1,0:T(8,128)(2,1)S(1)}, u32[]{:S(2)}, u32[]{:S(2)}) collective-permute-start(bf16[384,256]{1,0:T(8,128)(2,1)S(1)} %get-tuple-element.40), channel_id=1, source_target_pairs={{0,128},{128,256},{256,384},{384,512},{512,640},{640,768},{768,896... | collective-permute-start | bytes 589832 | tf_op jit(solution)/shard_map/ppermute | solution.py:308
  126.2 13.1 %collective-permute-start.10 = (bf16[384,256]{1,0:T(8,128)(2,1)S(1)}, bf16[384,256]{1,0:T(8,128)(2,1)S(1)}, u32[]{:S(2)}, u32[]{:S(2)}) collective-permute-start(bf16[384,256]{1,0:T(8,128)(2,1)S(1)} %get-tuple-element.41), channel_id=1, source_target_pairs={{0,896},{128,0},{256,128},{384,256},{512,384},{640,512},{768,640},... | collective-permute-start | bytes 589832 | tf_op jit(solution)/shard_map/ppermute | solution.py:308
  131.0 12.6 %collective-permute-start.14 = (bf16[384,256]{1,0:T(8,128)(2,1)S(1)}, bf16[384,256]{1,0:T(8,128)(2,1)S(1)}, u32[]{:S(2)}, u32[]{:S(2)}) collective-permute-start(bf16[384,256]{1,0:T(8,128)(2,1)S(1)} %get-tuple-element.47), channel_id=1, source_target_pairs={{0,256},{128,384},{256,512},{384,640},{512,768},{640,896},{768,0},... | collective-permute-start | bytes 589832 | tf_op jit(solution)/shard_map/ppermute | solution.py:308
  132.9 15.2 %collective-permute-start.15 = (bf16[384,256]{1,0:T(8,128)(2,1)S(1)}, bf16[384,256]{1,0:T(8,128)(2,1)S(1)}, u32[]{:S(2)}, u32[]{:S(2)}) collective-permute-start(bf16[384,256]{1,0:T(8,128)(2,1)S(1)} %get-tuple-element.48), channel_id=1, source_target_pairs={{0,768},{128,896},{256,0},{384,128},{512,256},{640,384},{768,512},... | collective-permute-start | bytes 589832 | tf_op jit(solution)/shard_map/ppermute | solution.py:308
where the time goes:
time: 150 us; the launch traced here: 149 us
  starting transfers between devices  90.3 us (60%)
  waiting for transfers between devices  37.8 us (25%)
  Pallas kernels  16.4 us (11%)
  local copies, waits for them, and re-layouts  3.54 us (2%)
    ppermute x14, starting transfers between devices, shifted(): return lax.ppermute(value, 'x', [(i, (i + by) % NX) for i in range(NX)])  45.5 us
    all_to_all x3, starting transfers between devices, exchange(): return lax.all_to_all(value, axis, split_axis=0, concat_axis=0, tiled=True)  36.6 us
    ppermute x14, waiting for transfers between devices, shifted(): return lax.ppermute(value, 'x', [(i, (i + by) % NX) for i in range(NX)])  19.3 us
    all_to_all x3, waiting for transfers between devices, exchange(): return lax.all_to_all(value, axis, split_axis=0, concat_axis=0, tiled=True)  15.4 us
    ppermute x1, starting transfers between devices, body(): oth = lax.ppermute(own, 'c', SWAP)  5.85 us
    unnamed x10, local copies, waits for them, and re-layouts  3.54 us
    ppermute x1, waiting for transfers between devices, body(): oth = lax.ppermute(own, 'c', SWAP)  3.06 us
  transfers between devices with their start and end apart: 19, of which 7 were waited for; matrix products, arithmetic and copies ran while one was open for 0% of the time, Pallas kernels for 6%

commit v1 on v0

--- a/solution.py
+++ b/solution.py
@@ -92,8 +92,7 @@
     out[0:BLK] = w_gate[...]
     out[BLK : 2 * BLK] = w_up[...]
     out[2 * BLK : 3 * BLK] = jnp.transpose(w_down[...].astype(f32)).astype(bf16)
-    lane = iota((8, HID), 1)
-    lane = jnp.where(lane < 16, lane & 7, 8).astype(f32)
+    lane = iota((8, HID), 1).astype(f32)
     hits = (column(routes[0:1]) == lane).astype(f32) + (column(routes[1:2]) == lane).astype(f32)
     total = jnp.sum(hits, axis=0, keepdims=True)
     row = iota((8, HID), 0)
@@ -194,7 +193,7 @@
         px.append(v.astype(bf16))
     to, fr = iota((256, 96), 0), iota((256, 96), 1)
     row, slot_of = to & 7, fr >> 5
-    same = 8 * ((to >> 3) & 3) + (to >> 5) == (fr & 31)
+    same = (to >> 3) == (fr & 31)
     first = one_hot(same & (row == 2 * slot_of))
     second = one_hot(same & (row == 2 * slot_of + 1))
     c60 = one_hot(same & (row == 6) & (slot_of == 0))
@@ -210,30 +209,14 @@
             k = k % 4
             return v[96 * j : 96 * j + 96, 256 * k : 256 * k + 256]
 
-        def store(v, lo, hi):
-            for y in range(8):
-                at = 64 * y + 32 * j
-                back[at : at + 32, lo:hi] = v[32 * y : 32 * y + 32]
-
         lo, hi = piece(6), piece(7)
         ends = ((c60, lo, c71, hi), (c60, hi, c72, lo), (c61, lo, c72, hi))
         for n in range(3):
             a, va, b, vb = ends[n]
             v = dot(first, piece(n)) + dot(second, piece(n + 3)) + dot(a, va) + dot(b, vb)
-            store(v.astype(bf16), 256 * n, 256 * n + 256)
+            back[256 * j : 256 * j + 256, 256 * n : 256 * n + 256] = v.astype(bf16)
         last = dot(for_dot, dots[96 * j : 96 * j + 96, :]) + jnp.where(count_at, tally, 0.0)
-        store(last.astype(bf16), 768, BACK)
-
-
-def sum_y(came, out):
-    s = came[0:64, :].astype(f32)
-    for k in range(1, 8):
-        s = s + came[64 * k : 64 * k + 64, :].astype(f32)
-    out[:, 0:768] = s[:, 0:768].astype(bf16)
-    last = s[:, 768:BACK]
-    high = jnp.floor(last * 0.0625)
-    digit = jnp.where(iota((64, BLK), 1) < 8, last - 16.0 * high, high)
-    out[:, 768:BACK] = jnp.where((iota((64, BLK), 0) & 7) == CAP, digit, last).astype(bf16)
+        back[256 * j : 256 * j + 256, 768:BACK] = last.astype(bf16)
 
 
 def weight_grads(x_rows, g_rows, grads, keep, send):
@@ -244,25 +227,35 @@
             ref[:, k * BLK : (k + 1) * BLK, :] = v.astype(bf16).reshape(8, BLK, HID)
 
 
-def add_cores(keep, came, *outs):
+def add_cores(keep, came, s0, s2, s4, s6, right, left):
     chip = lax.axis_index("x")
-    for k in range(8):
+
+    def total(k):
         at = lax.rem(chip + k, 8)
-        outs[k][...] = (keep[at].astype(f32) + came[at].astype(f32)).astype(bf16)
-
-
-def join(*refs):
-    s2, a, d, s6, b, t2, t6 = refs
-    t2[...] = (s2[...].astype(f32) + a[...].astype(f32) + d[...].astype(f32)).astype(bf16)
-    t6[...] = (s6[...].astype(f32) + b[...].astype(f32)).astype(bf16)
-
-
-def sum_chips(*refs):
-    ins, (gate, up, down) = refs[:5], refs[5:]
+        return (keep[at].astype(f32) + came[at].astype(f32)).astype(bf16)
+
+    right[0 : 3 * BLK] = total(3)
+    right[3 * BLK :] = total(1)
+    s4[...] = total(4)
+    left[0 : 3 * BLK] = total(5)
+    left[3 * BLK :] = total(7)
+    s2[...] = total(2)
+    s6[...] = total(6)
+    s0[...] = total(0)
+
+
+def join(s2, right, s4, s6, left, t2, t6):
+    far = slice(0, 3 * BLK)
+    t2[...] = (s2[...].astype(f32) + right[far].astype(f32) + s4[...].astype(f32)).astype(bf16)
+    t6[...] = (s6[...].astype(f32) + left[far].astype(f32)).astype(bf16)
+
+
+def sum_chips(s0, right, left, t2, t6, gate, up, down):
     for k, ref in ((0, gate), (1, up), (2, down)):
-        total = ins[0][k * BLK : (k + 1) * BLK].astype(f32)
-        for i in range(1, 5):
-            total = total + ins[i][k * BLK : (k + 1) * BLK].astype(f32)
+        lo, hi = k * BLK, (k + 1) * BLK
+        total = s0[lo:hi].astype(f32) + t2[lo:hi].astype(f32) + t6[lo:hi].astype(f32)
+        lo, hi = lo + 3 * BLK, hi + 3 * BLK
+        total = total + right[lo:hi].astype(f32) + left[lo:hi].astype(f32)
         ref[...] = (jnp.transpose(total) if k == 2 else total).astype(bf16)
 
 
@@ -274,8 +267,8 @@
     dots = []
     for x in range(2):
         s = jnp.zeros((8, BACK), f32)
-        for n in range(4):
-            at = 8 * (4 * x + n)
+        for n in range(32):
+            at = 8 * (32 * x + n)
             s = s + back[at : at + 8, :].astype(f32)
         counts = counts + s[CAP : CAP + 1, 768:BACK]
         at = slot[:, x : x + 1].astype(i32)
@@ -299,7 +292,7 @@
     lg = logits[...]
     e = jnp.exp(lg - jnp.max(lg, axis=1, keepdims=True))
     probs = e / jnp.sum(e, axis=1, keepdims=True)
-    cnt = counts[:, 0:8] + 16.0 * counts[:, 8:16]
+    cnt = counts[:, 0:8]
     target = 8.0 * (cnt / jnp.sum(cnt, axis=1, keepdims=True))
     aux_grad[...] = probs * (target - jnp.sum(probs * target, axis=1, keepdims=True))
 
@@ -344,21 +337,20 @@
     )(x_rows, g_rows, grads)
     other = lax.ppermute(send, "c", SWAP)
     back = call(row_grads, shape(8 * NSRC, BACK), 4)(grads, dots, own, oth)
-    back = exchange(back.reshape(NY, 8 * NZ, BACK), "y")
-    s = call(add_cores, tuple(shape(3 * BLK, HID) for _ in range(8)), 2)(keep, other)
-    a, d, b = shifted(s[3], 1), shifted(s[4], 2), shifted(s[5], 7)
-    e1 = shifted(s[1], 1)
-    e7 = shifted(s[7], 7)
-    t2, t6 = call(join, (shape(3 * BLK, HID), shape(3 * BLK, HID)), 5)(s[2], a, d, s[6], b)
-    e2, e6 = shifted(t2, 2), shifted(t6, 6)
-    back = call(sum_y, shape(8 * NZ, BACK), 1)(back.reshape(8 * NSRC, BACK))
-    back = exchange(back.reshape(NZ, 8, BACK), "z")
+    one, two = shape(3 * BLK, HID), shape(6 * BLK, HID)
+    s0, s2, s4, s6, right, left = call(add_cores, (one, one, one, one, two, two), 2)(keep, other)
+    right = shifted(right, 1)
+    s4 = shifted(s4, 2)
+    left = shifted(left, 7)
+    back = exchange(back.reshape(NSRC, 8, BACK), ("z", "y"))
+    t2, t6 = call(join, (one, one), 5)(s2, right, s4, s6, left)
+    t2, t6 = shifted(t2, 2), shifted(t6, 6)
     grad_gate, grad_up, grad_down = call(
         sum_chips, (shape(BLK, HID), shape(BLK, HID), shape(HID, BLK)), 5
-    )(s[0], e1, e7, e2, e6)
+    )(s0, right, left, t2, t6)
     grad_tokens, route_dot, aux_grad = call(
         finish, (shape(8, DM), shape(2, 8, dtype=f32), shape(8, 8, dtype=f32)), 3
-    )(back.reshape(8 * NZ, BACK), routes_t, logits)
+    )(back.reshape(8 * NSRC, BACK), routes_t, logits)
     return (grad_tokens, route_dot.T, aux_grad, grad_gate, grad_up, grad_down)
 
 

time: 150 us -> 138 us (0.920)
  the two profiles are of different devices: /device:TPU:1 before, /device:TPU:4 now
where the time goes in v1:
time: 138 us; the launch traced here: 137 us
  starting transfers between devices  85.7 us (62%)
  waiting for transfers between devices  32.3 us (23%)
  Pallas kernels  14.9 us (11%)
  local copies, waits for them, and re-layouts  3.57 us (3%)
    ppermute x12, starting transfers between devices, shifted(): return lax.ppermute(value, 'x', [(i, (i + by) % NX) for i in range(NX)])  45.9 us
    all_to_all x2, starting transfers between devices, exchange(): return lax.all_to_all(value, axis, split_axis=0, concat_axis=0, tiled=True)  35.8 us
    ppermute x12, waiting for transfers between devices, shifted(): return lax.ppermute(value, 'x', [(i, (i + by) % NX) for i in range(NX)])  28.8 us
    unnamed x10, local copies, waits for them, and re-layouts  3.57 us
    ppermute x1, waiting for transfers between devices, body(): oth = lax.ppermute(own, 'c', SWAP)  3.42 us
  transfers between devices with their start and end apart: 16, of which 7 were waited for; matrix products, arithmetic and copies ran while one was open for 0% of the time, Pallas kernels for 5%

profile of v1, /device:TPU:4, one launch (start us, length us, event | category | flops | bytes accessed | tf_op | source)
XLA Modules:
  0.0 137.3 jit_solution(4755271110633265722)
XLA Ops:
  0.6 2.8 %shard_map.118 = bf16[64,8,1536]{2,1,0:T(8,128)(2,1)} custom-call(bf16[8,2048]{1,0:T(8,128)(2,1)} %tokens.1, bf16[8,2048]{1,0:T(8,128)(2,1)} %cotangent.1, s32[2,8]{1,0:T(2,128)} %bitcast.7, f32[8,8]{1,0:T(8,128)} %logits.3), custom_call_target="tpu_custom_call" | custom-call | tf_op jit(solution)/shard_map/pallas_call | solution.py:313
  3.4 23.4 %all-to-all-start = ((bf16[64,8,1536]{2,1,0:T(8,128)(2,1)}), bf16[64,8,1536]{2,1,0:T(8,128)(2,1)S(1)}, u32[]{:S(2)}, u32[]{:S(2)}) async-start(bf16[64,8,1536]{2,1,0:T(8,128)(2,1)} %shard_map.118), calls=%async_computation | async-start | bytes 3145728 | tf_op jit(solution)/shard_map/all_to_all | solution.py:305
  26.8 1.7 %shard_map.119.refs_0_ = bf16[392,256]{1,0:T(8,128)(2,1)} custom-call(s32[2,8]{1,0:T(2,128)} %bitcast.8, bf16[128,256]{1,0:T(8,128)(2,1)} %w_gate.1, bf16[128,256]{1,0:T(8,128)(2,1)} %w_up.1, bf16[256,128]{1,0:T(8,128)(2,1)} %w_down.1), custom_call_target="tpu_custom_call" | custom-call | tf_op jit(solution)/shard_map/pallas_call | solution.py:310
  28.5 2.4 %collective-permute-start.4 = (bf16[392,256]{1,0:T(8,128)(2,1)}, bf16[392,256]{1,0:T(8,128)(2,1)S(1)}, u32[]{:S(2)}, u32[]{:S(2)}) collective-permute-start(bf16[392,256]{1,0:T(8,128)(2,1)} %shard_map.119.refs_0_), channel_id=1, source_target_pairs={{0,768},{128,896},{256,0},{384,128},{512,256},{640,384},{768,512},... | collective-permute-start | bytes 602120 | tf_op jit(solution)/shard_map/ppermute | solution.py:301
  30.9 5.5 %collective-permute-start.1 = (bf16[392,256]{1,0:T(8,128)(2,1)}, bf16[392,256]{1,0:T(8,128)(2,1)S(1)}, u32[]{:S(2)}, u32[]{:S(2)}) collective-permute-start(bf16[392,256]{1,0:T(8,128)(2,1)} %shard_map.119.refs_0_), channel_id=1, source_target_pairs={{0,256},{128,384},{256,512},{384,640},{512,768},{640,896},{768,0},... | collective-permute-start | bytes 602120 | tf_op jit(solution)/shard_map/ppermute | solution.py:301
  36.5 1.9 %collective-permute-start.6 = (bf16[392,256]{1,0:T(8,128)(2,1)}, bf16[392,256]{1,0:T(8,128)(2,1)S(1)}, u32[]{:S(2)}, u32[]{:S(2)}) collective-permute-start(bf16[392,256]{1,0:T(8,128)(2,1)} %shard_map.119.refs_0_), channel_id=1, source_target_pairs={{0,896},{128,0},{256,128},{384,256},{512,384},{640,512},{768,640},... | collective-permute-start | bytes 602120 | tf_op jit(solution)/shard_map/ppermute | solution.py:301
  38.4 3.9 %collective-permute-start = (bf16[392,256]{1,0:T(8,128)(2,1)}, bf16[392,256]{1,0:T(8,128)(2,1)S(1)}, u32[]{:S(2)}, u32[]{:S(2)}) collective-permute-start(bf16[392,256]{1,0:T(8,128)(2,1)} %shard_map.119.refs_0_), channel_id=1, source_target_pairs={{0,128},{128,256},{256,384},{384,512},{512,640},{640,768},{768,896... | collective-permute-start | bytes 602120 | tf_op jit(solution)/shard_map/ppermute | solution.py:301
  42.3 2.2 %collective-permute-done.4.refs_6_ = bf16[392,256]{1,0:T(8,128)(2,1)S(1)} collective-permute-done((bf16[392,256]{1,0:T(8,128)(2,1)}, bf16[392,256]{1,0:T(8,128)(2,1)S(1)}, u32[]{:S(2)}, u32[]{:S(2)}) %collective-permute-start.4) | collective-permute-done | bytes 200736 | tf_op jit(solution)/shard_map/ppermute | solution.py:301
  44.5 1.9 %collective-permute-start.5 = (bf16[392,256]{1,0:T(8,128)(2,1)S(1)}, bf16[392,256]{1,0:T(8,128)(2,1)S(1)}, u32[]{:S(2)}, u32[]{:S(2)}) collective-permute-start(bf16[392,256]{1,0:T(8,128)(2,1)S(1)} %collective-permute-done.4.refs_6_), channel_id=1, source_target_pairs={{0,896},{128,0},{256,128},{384,256},{512,384},{640,512},{768,640},... | collective-permute-start | bytes 602120 | tf_op jit(solution)/shard_map/ppermute | solution.py:301
  46.4 5.1 %collective-permute-start.3 = (bf16[392,256]{1,0:T(8,128)(2,1)S(1)}, bf16[392,256]{1,0:T(8,128)(2,1)S(1)}, u32[]{:S(2)}, u32[]{:S(2)}) collective-permute-start(bf16[392,256]{1,0:T(8,128)(2,1)S(1)} %collective-permute-done.1.refs_2_), channel_id=1, source_target_pairs={{0,256},{128,384},{256,512},{384,640},{512,768},{640,896},{768,0},... | collective-permute-start | bytes 602120 | tf_op jit(solution)/shard_map/ppermute | solution.py:301
  51.6 3.0 %collective-permute-start.2 = (bf16[392,256]{1,0:T(8,128)(2,1)S(1)}, bf16[392,256]{1,0:T(8,128)(2,1)S(1)}, u32[]{:S(2)}, u32[]{:S(2)}) collective-permute-start(bf16[392,256]{1,0:T(8,128)(2,1)S(1)} %collective-permute-done.1.refs_2_), channel_id=1, source_target_pairs={{0,128},{128,256},{256,384},{384,512},{512,640},{640,768},{768,896... | collective-permute-start | bytes 602120 | tf_op jit(solution)/shard_map/ppermute | solution.py:301
  54.7 5.7 %collective-permute-done.3.refs_4_ = bf16[392,256]{1,0:T(8,128)(2,1)S(1)} collective-permute-done((bf16[392,256]{1,0:T(8,128)(2,1)S(1)}, bf16[392,256]{1,0:T(8,128)(2,1)S(1)}, u32[]{:S(2)}, u32[]{:S(2)}) %collective-permute-start.3) | collective-permute-done | bytes 200736 | tf_op jit(solution)/shard_map/ppermute | solution.py:301
  60.4 2.6 %collective-permute-done.2.refs_3_ = bf16[392,256]{1,0:T(8,128)(2,1)S(1)} collective-permute-done((bf16[392,256]{1,0:T(8,128)(2,1)S(1)}, bf16[392,256]{1,0:T(8,128)(2,1)S(1)}, u32[]{:S(2)}, u32[]{:S(2)}) %collective-permute-start.2) | collective-permute-done | bytes 200736 | tf_op jit(solution)/shard_map/ppermute | solution.py:301
  64.0 1.9 %collective-permute-start.7 = (bf16[8,392,256]{2,1,0:T(8,128)(2,1)S(1)}, bf16[8,392,256]{2,1,0:T(8,128)(2,1)S(1)}, u32[]{:S(2)}, u32[]{:S(2)}) collective-permute-start(bf16[8,392,256]{2,1,0:T(8,128)(2,1)S(1)} %shard_map.120.own), channel_id=1, source_target_pairs={{0,64},{64,0},{1,65},{65,1},{2,66},{66,2},{3,67},{67,3},{4,68},{68... | collective-permute-start | bytes 4816904 | tf_op jit(solution)/shard_map/ppermute | solution.py:321
  65.9 3.4 %collective-permute-done.7.far = bf16[8,392,256]{2,1,0:T(8,128)(2,1)S(1)} collective-permute-done((bf16[8,392,256]{2,1,0:T(8,128)(2,1)S(1)}, bf16[8,392,256]{2,1,0:T(8,128)(2,1)S(1)}, u32[]{:S(2)}, u32[]{:S(2)}) %collective-permute-start.7) | collective-permute-done | bytes 1605664 | tf_op jit(solution)/shard_map/ppermute | solution.py:321
  69.3 1.2 copy-done
  70.5 1.4 %copy-done.1 = bf16[8,392,256]{2,1,0:T(8,128)(2,1)S(1)} copy-done((bf16[8,392,256]{2,1,0:T(8,128)(2,1)S(1)}, bf16[8,392,256]{2,1,0:T(8,128)(2,1)}, u32[]{:S(2)}) %copy-start.1) | copy-done | bytes 1605656
  72.0 2.1 %shard_map.121 = (bf16[192,2048]{1,0:T(8,128)(2,1)S(1)}, bf16[192,2048]{1,0:T(8,128)(2,1)S(1)}, bf16[192,768]{1,0:T(8,128)(2,1)S(1)}, bf16[192,128]{1,0:T(8,128)(2,1)S(1)}, bf16[8,392,256]{2,1,0:T(8,128)(2,1)S(1)}) custom-call(bf16[512,1536]{1,0:T(8,128)(2,1)S(1)} %bitcast.5, bf16[8,392,256]{2,1,0:T(8,128)(2,1)S(1)} %shard_map.120.own, ...), custom_call_target="tpu_custom_call" | custom-call | tf_op jit(solution)/shard_map/pallas_call | solution.py:322
  74.1 2.0 %shard_map.124 = (bf16[8,384,256]{2,1,0:T(8,128)(2,1)S(1)}, bf16[8,384,256]{2,1,0:T(8,128)(2,1)}) custom-call(bf16[192,2048]{1,0:T(8,128)(2,1)S(1)} %get-tuple-element.33.x_rows, bf16[192,2048]{1,0:T(8,128)(2,1)S(1)} %get-tuple-element.34.g_rows, bf16[192,768]{1,0:T(8,128)(2,1)S(1)} %get-tuple-element.27.grads), custom_call_target="tpu_custom_call" | custom-call | tf_op jit(solution)/shard_map/pallas_call | solution.py:335
  76.1 2.0 %collective-permute-start.8 = (bf16[8,384,256]{2,1,0:T(8,128)(2,1)}, bf16[8,384,256]{2,1,0:T(8,128)(2,1)}, u32[]{:S(2)}, u32[]{:S(2)}) collective-permute-start(bf16[8,384,256]{2,1,0:T(8,128)(2,1)} %get-tuple-element.36), channel_id=1, source_target_pairs={{0,64},{64,0},{1,65},{65,1},{2,66},{66,2},{3,67},{67,3},{4,68},{68... | collective-permute-start | bytes 4718600 | tf_op jit(solution)/shard_map/ppermute | solution.py:338
  78.1 2.6 %shard_map.122 = bf16[512,896]{1,0:T(8,128)(2,1)} custom-call(bf16[192,768]{1,0:T(8,128)(2,1)S(1)} %get-tuple-element.27.grads, bf16[192,128]{1,0:T(8,128)(2,1)S(1)} %get-tuple-element.28.dots, bf16[8,392,256]{2,1,0:T(8,128)(2,1)S(1)} %shard_map.120.own, bf16[8,392,256]{2,1,0:T(8,128)(2,1)S(1)} %get-tuple-element.29.oth), custom_call_target="tpu_custom_call" | custom-call | tf_op jit(solution)/shard_map/pallas_call | solution.py:339
  80.8 12.4 %all-to-all-start.1 = ((bf16[64,8,896]{2,1,0:T(8,128)(2,1)}), bf16[64,8,896]{2,1,0:T(8,128)(2,1)S(1)}, u32[]{:S(2)}, u32[]{:S(2)}) async-start(bf16[64,8,896]{2,1,0:T(8,128)(2,1)} %bitcast.2), calls=%async_computation.1 | async-start | bytes 1835008 | tf_op jit(solution)/shard_map/all_to_all | solution.py:305
  93.2 1.8 %shard_map.125 = (bf16[384,256]{1,0:T(8,128)(2,1)S(1)}, bf16[384,256]{1,0:T(8,128)(2,1)S(1)}, bf16[384,256]{1,0:T(8,128)(2,1)S(1)}, bf16[384,256]{1,0:T(8,128)(2...) custom-call(bf16[8,384,256]{2,1,0:T(8,128)(2,1)S(1)} %get-tuple-element.35.keep, ...), custom_call_target="tpu_custom_call" | custom-call | tf_op jit(solution)/shard_map/pallas_call | solution.py:341
  95.0 3.8 %collective-permute-start.9 = (bf16[768,256]{1,0:T(8,128)(2,1)S(1)}, bf16[768,256]{1,0:T(8,128)(2,1)S(1)}, u32[]{:S(2)}, u32[]{:S(2)}) collective-permute-start(bf16[768,256]{1,0:T(8,128)(2,1)S(1)} %get-tuple-element.38), channel_id=1, source_target_pairs={{0,128},{128,256},{256,384},{384,512},{512,640},{640,768},{768,896... | collective-permute-start | bytes 1179656 | tf_op jit(solution)/shard_map/ppermute | solution.py:301
  98.8 2.0 %collective-permute-start.10 = (bf16[768,256]{1,0:T(8,128)(2,1)S(1)}, bf16[768,256]{1,0:T(8,128)(2,1)S(1)}, u32[]{:S(2)}, u32[]{:S(2)}) collective-permute-start(bf16[768,256]{1,0:T(8,128)(2,1)S(1)} %get-tuple-element.39), channel_id=1, source_target_pairs={{0,896},{128,0},{256,128},{384,256},{512,384},{640,512},{768,640},... | collective-permute-start | bytes 1179656 | tf_op jit(solution)/shard_map/ppermute | solution.py:301
  100.8 7.7 %collective-permute-start.11 = (bf16[384,256]{1,0:T(8,128)(2,1)S(1)}, bf16[384,256]{1,0:T(8,128)(2,1)S(1)}, u32[]{:S(2)}, u32[]{:S(2)}) collective-permute-start(bf16[384,256]{1,0:T(8,128)(2,1)S(1)} %get-tuple-element.41), channel_id=1, source_target_pairs={{0,256},{128,384},{256,512},{384,640},{512,768},{640,896},{768,0},... | collective-permute-start | bytes 589832 | tf_op jit(solution)/shard_map/ppermute | solution.py:301
  108.5 7.4 %collective-permute-done.11.s4 = bf16[384,256]{1,0:T(8,128)(2,1)S(1)} collective-permute-done((bf16[384,256]{1,0:T(8,128)(2,1)S(1)}, bf16[384,256]{1,0:T(8,128)(2,1)S(1)}, u32[]{:S(2)}, u32[]{:S(2)}) %collective-permute-start.11) | collective-permute-done | bytes 196640 | tf_op jit(solution)/shard_map/ppermute | solution.py:301
  116.1 6.6 %collective-permute-start.12 = (bf16[384,256]{1,0:T(8,128)(2,1)S(1)}, bf16[384,256]{1,0:T(8,128)(2,1)S(1)}, u32[]{:S(2)}, u32[]{:S(2)}) collective-permute-start(bf16[384,256]{1,0:T(8,128)(2,1)S(1)} %get-tuple-element.43), channel_id=1, source_target_pairs={{0,256},{128,384},{256,512},{384,640},{512,768},{640,896},{768,0},... | collective-permute-start | bytes 589832 | tf_op jit(solution)/shard_map/ppermute | solution.py:301
  122.7 1.9 %collective-permute-start.13 = (bf16[384,256]{1,0:T(8,128)(2,1)S(1)}, bf16[384,256]{1,0:T(8,128)(2,1)S(1)}, u32[]{:S(2)}, u32[]{:S(2)}) collective-permute-start(bf16[384,256]{1,0:T(8,128)(2,1)S(1)} %get-tuple-element.44), channel_id=1, source_target_pairs={{0,768},{128,896},{256,0},{384,128},{512,256},{640,384},{768,512},... | collective-permute-start | bytes 589832 | tf_op jit(solution)/shard_map/ppermute | solution.py:301
  124.6 0.9 shard_map.123
  125.6 4.3 %collective-permute-done.12.t2 = bf16[384,256]{1,0:T(8,128)(2,1)S(1)} collective-permute-done((bf16[384,256]{1,0:T(8,128)(2,1)S(1)}, bf16[384,256]{1,0:T(8,128)(2,1)S(1)}, u32[]{:S(2)}, u32[]{:S(2)}) %collective-permute-start.12) | collective-permute-done | bytes 196640 | tf_op jit(solution)/shard_map/ppermute | solution.py:301
  129.8 6.7 %collective-permute-done.13.t6 = bf16[384,256]{1,0:T(8,128)(2,1)S(1)} collective-permute-done((bf16[384,256]{1,0:T(8,128)(2,1)S(1)}, bf16[384,256]{1,0:T(8,128)(2,1)S(1)}, u32[]{:S(2)}, u32[]{:S(2)}) %collective-permute-start.13) | collective-permute-done | bytes 196640 | tf_op jit(solution)/shard_map/ppermute | solution.py:301
  (20 shorter events, 2.0 us)
Async XLA Ops:
  3.4 67.2 %all-to-all-start = ((bf16[64,8,1536]{2,1,0:T(8,128)(2,1)}), bf16[64,8,1536]{2,1,0:T(8,128)(2,1)S(1)}, u32[]{:S(2)}, u32[]{:S(2)}) async-start(bf16[64,8,1536]{2,1,0:T(8,128)(2,1)} %shard_map.118), calls=%async_computation | async-start | bytes 3145728 | tf_op jit(solution)/shard_map/all_to_all | solution.py:305
  28.5 16.0 %collective-permute-start.4 = (bf16[392,256]{1,0:T(8,128)(2,1)}, bf16[392,256]{1,0:T(8,128)(2,1)S(1)}, u32[]{:S(2)}, u32[]{:S(2)}) collective-permute-start(bf16[392,256]{1,0:T(8,128)(2,1)} %shard_map.119.refs_0_), channel_id=1, source_target_pairs={{0,768},{128,896},{256,0},{384,128},{512,256},{640,384},{768,512},... | collective-permute-start | bytes 602120 | tf_op jit(solution)/shard_map/ppermute | solution.py:301
  30.9 15.5 %collective-permute-start.1 = (bf16[392,256]{1,0:T(8,128)(2,1)}, bf16[392,256]{1,0:T(8,128)(2,1)S(1)}, u32[]{:S(2)}, u32[]{:S(2)}) collective-permute-start(bf16[392,256]{1,0:T(8,128)(2,1)} %shard_map.119.refs_0_), channel_id=1, source_target_pairs={{0,256},{128,384},{256,512},{384,640},{512,768},{640,896},{768,0},... | collective-permute-start | bytes 602120 | tf_op jit(solution)/shard_map/ppermute | solution.py:301
  36.5 18.2 %collective-permute-start.6 = (bf16[392,256]{1,0:T(8,128)(2,1)}, bf16[392,256]{1,0:T(8,128)(2,1)S(1)}, u32[]{:S(2)}, u32[]{:S(2)}) collective-permute-start(bf16[392,256]{1,0:T(8,128)(2,1)} %shard_map.119.refs_0_), channel_id=1, source_target_pairs={{0,896},{128,0},{256,128},{384,256},{512,384},{640,512},{768,640},... | collective-permute-start | bytes 602120 | tf_op jit(solution)/shard_map/ppermute | solution.py:301
  38.4 16.2 %collective-permute-start = (bf16[392,256]{1,0:T(8,128)(2,1)}, bf16[392,256]{1,0:T(8,128)(2,1)S(1)}, u32[]{:S(2)}, u32[]{:S(2)}) collective-permute-start(bf16[392,256]{1,0:T(8,128)(2,1)} %shard_map.119.refs_0_), channel_id=1, source_target_pairs={{0,128},{128,256},{256,384},{384,512},{512,640},{640,768},{768,896... | collective-permute-start | bytes 602120 | tf_op jit(solution)/shard_map/ppermute | solution.py:301
  44.5 10.2 %collective-permute-start.5 = (bf16[392,256]{1,0:T(8,128)(2,1)S(1)}, bf16[392,256]{1,0:T(8,128)(2,1)S(1)}, u32[]{:S(2)}, u32[]{:S(2)}) collective-permute-start(bf16[392,256]{1,0:T(8,128)(2,1)S(1)} %collective-permute-done.4.refs_6_), channel_id=1, source_target_pairs={{0,896},{128,0},{256,128},{384,256},{512,384},{640,512},{768,640},... | collective-permute-start | bytes 602120 | tf_op jit(solution)/shard_map/ppermute | solution.py:301
  46.4 13.9 %collective-permute-start.3 = (bf16[392,256]{1,0:T(8,128)(2,1)S(1)}, bf16[392,256]{1,0:T(8,128)(2,1)S(1)}, u32[]{:S(2)}, u32[]{:S(2)}) collective-permute-start(bf16[392,256]{1,0:T(8,128)(2,1)S(1)} %collective-permute-done.1.refs_2_), channel_id=1, source_target_pairs={{0,256},{128,384},{256,512},{384,640},{512,768},{640,896},{768,0},... | collective-permute-start | bytes 602120 | tf_op jit(solution)/shard_map/ppermute | solution.py:301
  51.6 11.4 %collective-permute-start.2 = (bf16[392,256]{1,0:T(8,128)(2,1)S(1)}, bf16[392,256]{1,0:T(8,128)(2,1)S(1)}, u32[]{:S(2)}, u32[]{:S(2)}) collective-permute-start(bf16[392,256]{1,0:T(8,128)(2,1)S(1)} %collective-permute-done.1.refs_2_), channel_id=1, source_target_pairs={{0,128},{128,256},{256,384},{384,512},{512,640},{640,768},{768,896... | collective-permute-start | bytes 602120 | tf_op jit(solution)/shard_map/ppermute | solution.py:301
  62.9 0.9 copy-start.2
  64.0 5.4 %collective-permute-start.7 = (bf16[8,392,256]{2,1,0:T(8,128)(2,1)S(1)}, bf16[8,392,256]{2,1,0:T(8,128)(2,1)S(1)}, u32[]{:S(2)}, u32[]{:S(2)}) collective-permute-start(bf16[8,392,256]{2,1,0:T(8,128)(2,1)S(1)} %shard_map.120.own), channel_id=1, source_target_pairs={{0,64},{64,0},{1,65},{65,1},{2,66},{66,2},{3,67},{67,3},{4,68},{68... | collective-permute-start | bytes 4816904 | tf_op jit(solution)/shard_map/ppermute | solution.py:321
  69.3 1.2 copy-start
  70.5 1.4 %copy-start.1 = (bf16[8,392,256]{2,1,0:T(8,128)(2,1)S(1)}, bf16[8,392,256]{2,1,0:T(8,128)(2,1)}, u32[]{:S(2)}) copy-start(bf16[8,392,256]{2,1,0:T(8,128)(2,1)} %copy-done) | copy-start | bytes 4816900
  76.1 17.1 %collective-permute-start.8 = (bf16[8,384,256]{2,1,0:T(8,128)(2,1)}, bf16[8,384,256]{2,1,0:T(8,128)(2,1)}, u32[]{:S(2)}, u32[]{:S(2)}) collective-permute-start(bf16[8,384,256]{2,1,0:T(8,128)(2,1)} %get-tuple-element.36), channel_id=1, source_target_pairs={{0,64},{64,0},{1,65},{65,1},{2,66},{66,2},{3,67},{67,3},{4,68},{68... | collective-permute-start | bytes 4718600 | tf_op jit(solution)/shard_map/ppermute | solution.py:338
  80.8 43.8 %all-to-all-start.1 = ((bf16[64,8,896]{2,1,0:T(8,128)(2,1)}), bf16[64,8,896]{2,1,0:T(8,128)(2,1)S(1)}, u32[]{:S(2)}, u32[]{:S(2)}) async-start(bf16[64,8,896]{2,1,0:T(8,128)(2,1)} %bitcast.2), calls=%async_computation.1 | async-start | bytes 1835008 | tf_op jit(solution)/shard_map/all_to_all | solution.py:305
  93.2 31.4 %copy-start.3 = (f32[8,8]{1,0:T(8,128)S(1)}, f32[8,8]{1,0:T(8,128)}, u32[]{:S(2)}) copy-start(f32[8,8]{1,0:T(8,128)} %logits.3) | copy-start | bytes 772
  93.2 31.4 %copy-start.4 = (s32[8,2]{0,1:T(2,128)S(1)}, s32[8,2]{0,1:T(2,128)}, u32[]{:S(2)}) copy-start(s32[8,2]{0,1:T(2,128)} %param.9) | copy-start | bytes 196
  95.0 21.0 %collective-permute-start.9 = (bf16[768,256]{1,0:T(8,128)(2,1)S(1)}, bf16[768,256]{1,0:T(8,128)(2,1)S(1)}, u32[]{:S(2)}, u32[]{:S(2)}) collective-permute-start(bf16[768,256]{1,0:T(8,128)(2,1)S(1)} %get-tuple-element.38), channel_id=1, source_target_pairs={{0,128},{128,256},{256,384},{384,512},{512,640},{640,768},{768,896... | collective-permute-start | bytes 1179656 | tf_op jit(solution)/shard_map/ppermute | solution.py:301
  98.8 17.1 %collective-permute-start.10 = (bf16[768,256]{1,0:T(8,128)(2,1)S(1)}, bf16[768,256]{1,0:T(8,128)(2,1)S(1)}, u32[]{:S(2)}, u32[]{:S(2)}) collective-permute-start(bf16[768,256]{1,0:T(8,128)(2,1)S(1)} %get-tuple-element.39), channel_id=1, source_target_pairs={{0,896},{128,0},{256,128},{384,256},{512,384},{640,512},{768,640},... | collective-permute-start | bytes 1179656 | tf_op jit(solution)/shard_map/ppermute | solution.py:301
  100.8 15.1 %collective-permute-start.11 = (bf16[384,256]{1,0:T(8,128)(2,1)S(1)}, bf16[384,256]{1,0:T(8,128)(2,1)S(1)}, u32[]{:S(2)}, u32[]{:S(2)}) collective-permute-start(bf16[384,256]{1,0:T(8,128)(2,1)S(1)} %get-tuple-element.41), channel_id=1, source_target_pairs={{0,256},{128,384},{256,512},{384,640},{512,768},{640,896},{768,0},... | collective-permute-start | bytes 589832 | tf_op jit(solution)/shard_map/ppermute | solution.py:301
  116.1 13.8 %collective-permute-start.12 = (bf16[384,256]{1,0:T(8,128)(2,1)S(1)}, bf16[384,256]{1,0:T(8,128)(2,1)S(1)}, u32[]{:S(2)}, u32[]{:S(2)}) collective-permute-start(bf16[384,256]{1,0:T(8,128)(2,1)S(1)} %get-tuple-element.43), channel_id=1, source_target_pairs={{0,256},{128,384},{256,512},{384,640},{512,768},{640,896},{768,0},... | collective-permute-start | bytes 589832 | tf_op jit(solution)/shard_map/ppermute | solution.py:301
  122.7 13.9 %collective-permute-start.13 = (bf16[384,256]{1,0:T(8,128)(2,1)S(1)}, bf16[384,256]{1,0:T(8,128)(2,1)S(1)}, u32[]{:S(2)}, u32[]{:S(2)}) collective-permute-start(bf16[384,256]{1,0:T(8,128)(2,1)S(1)} %get-tuple-element.44), channel_id=1, source_target_pairs={{0,768},{128,896},{256,0},{384,128},{512,256},{640,384},{768,512},... | collective-permute-start | bytes 589832 | tf_op jit(solution)/shard_map/ppermute | solution.py:301

commit v2 on v1

--- a/solution.py
+++ b/solution.py
@@ -15,10 +15,10 @@
 HID = 256
 BLK = 128
 NSRC = NZ * NY
-WIRE = 1536
 BACK = 896
 SHARD = 3 * BLK + 8
 ROWS = NSRC * CAP
+HELD = (2, 6)
 VM = pl.BlockSpec(memory_space=pltpu.VMEM)
 FAR = pl.BlockSpec(memory_space=pltpu.HBM)
 bf16, f32, i32 = jnp.bfloat16, jnp.float32, jnp.int32
@@ -118,22 +118,28 @@
         sel_x = jnp.where((at == lane) & (lane < CAP), mem, 0.0).astype(bf16)
         sel_g = jnp.where((at + CAP == lane) & (lane < 2 * CAP), mem, 0.0).astype(bf16)
         grads = (cot * scaled[:, x : x + 1]).astype(bf16)
-        rows = dot(sel_x, tok_b, FIRST) + dot(sel_g, grads, FIRST)
-        tail = rows[:, WIRE:].astype(bf16)
-        pieces = []
-        for r in range(CAP):
-            to, fr = iota((8, 8), 0), iota((8, 8), 1)
-            move = ((to == 6) & (fr == r)) | ((to == 7) & (fr == CAP + r))
-            moved = dot(move.astype(f32).astype(bf16), tail)
-            pieces.append((rows[:, 512 * r : 512 * r + 512] + moved).astype(bf16))
-        block = jnp.concatenate(pieces, axis=1)
-        out[32 * x : 32 * x + 32] = jnp.broadcast_to(block[None], (32, 8, WIRE))
+        block = (dot(sel_x, tok_b, FIRST) + dot(sel_g, grads, FIRST)).astype(bf16)
+        out[4 * x : 4 * x + 4] = jnp.broadcast_to(block[None], (4, 8, DM))
+
+
+def repack(came, out):
+    to, fr = iota((48, 64), 0), iota((48, 64), 1)
+    block = dot(one_hot(fr == 8 * (to & 7) + (to >> 3)), came[...]).astype(bf16)
+    out[...] = jnp.broadcast_to(block[None], (NY, 48, DM))
 
 
 def stack_shards(*refs):
-    out, chip = refs[8], lax.axis_index("x")
+    out, sem, chip = refs[8], refs[9], lax.axis_index("x")
+    fetches = []
+    for n, k in enumerate(HELD):
+        at = lax.rem(chip + 8 - k, 8)
+        fetches.append(pltpu.make_async_copy(refs[k], out.at[at], sem.at[n]))
+        fetches[-1].start()
     for k in range(8):
-        out[lax.rem(chip + 8 - k, 8)] = refs[k][...]
+        if k not in HELD:
+            out[lax.rem(chip + 8 - k, 8)] = refs[k][...]
+    for fetch in fetches:
+        fetch.wait()
 
 
 def one_hot(cond):
@@ -144,28 +150,21 @@
     return ref[:, k * BLK : (k + 1) * BLK, :].reshape(DM // 2, HID)
 
 
-def forward(wire, own, far, x_out, g_out, grads_out, dots_out, oth, sem):
+def unpack(came, x_out, g_out):
+    for y in range(NY):
+        x_out[24 * y : 24 * y + 24] = came[48 * y : 48 * y + 24]
+        g_out[24 * y : 24 * y + 24] = came[48 * y + 24 : 48 * y + 48]
+
+
+def forward(x_rows, g_rows, own, far, grads_out, dots_out, oth, sem):
     fetch = pltpu.make_async_copy(far, oth, sem)
     fetch.start()
-    to, fr = iota((192, 256), 0), iota((192, 256), 1)
-    main = one_hot(fr == 8 * (to & 31) + (to >> 5))
-    to, fr = iota((64, 256), 0), iota((64, 256), 1)
-    ends = one_hot(fr == 8 * (to & 31) + 6 + (to >> 5))
-    for j in range(2):
-        part = dot(main, wire[256 * j : 256 * j + 256, :]).astype(bf16)
-        x_out[96 * j : 96 * j + 96, 0:WIRE] = part[0:96]
-        g_out[96 * j : 96 * j + 96, 0:WIRE] = part[96:192]
-        for r in range(CAP):
-            at = 96 * j + 32 * r
-            tail = dot(ends, wire[256 * j : 256 * j + 256, 512 * r : 512 * r + 512]).astype(bf16)
-            x_out[at : at + 32, WIRE:DM] = tail[0:32]
-            g_out[at : at + 32, WIRE:DM] = tail[32:64]
     half = DM // 2
-    near = [dot(rows[:, 0:half], weight(own, k)) for k, rows in enumerate((x_out, x_out, g_out))]
+    near = [dot(rows[:, 0:half], weight(own, k)) for k, rows in enumerate((x_rows, x_rows, g_rows))]
     fetch.wait()
     gate_pre, up_pre, hidden_grad = [
         near[k] + dot(rows[:, half:DM], weight(oth, k))
-        for k, rows in enumerate((x_out, x_out, g_out))
+        for k, rows in enumerate((x_rows, x_rows, g_rows))
     ]
     sigma = 1.0 / (1.0 + jnp.exp(-gate_pre))
     active = gate_pre * sigma
@@ -192,15 +191,16 @@
         v = dot(gate_grad, weight(ref, 0), LAST) + dot(up_grad, weight(ref, 1), LAST)
         px.append(v.astype(bf16))
     to, fr = iota((256, 96), 0), iota((256, 96), 1)
-    row, slot_of = to & 7, fr >> 5
-    same = (to >> 3) == (fr & 31)
-    first = one_hot(same & (row == 2 * slot_of))
-    second = one_hot(same & (row == 2 * slot_of + 1))
-    c60 = one_hot(same & (row == 6) & (slot_of == 0))
-    c61 = one_hot(same & (row == 6) & (slot_of == 1))
-    c71 = one_hot(same & (row == 7) & (slot_of == 1))
-    c72 = one_hot(same & (row == 7) & (slot_of == 2))
-    for_dot = one_hot(same & (row == slot_of))
+    row = to & 7
+    base = fr - 24 * ((to >> 3) & 3) - (to >> 5)
+    paired = (row < 6) & (base == 8 * (row >> 1))
+    first = one_hot(paired & ((row & 1) == 0))
+    second = one_hot(paired & ((row & 1) == 1))
+    c60 = one_hot((row == 6) & (base == 0))
+    c61 = one_hot((row == 6) & (base == 8))
+    c71 = one_hot((row == 7) & (base == 8))
+    c72 = one_hot((row == 7) & (base == 16))
+    for_dot = one_hot((row < CAP) & (base == 8 * row))
     count_at = (iota((256, BLK), 0) & 7) == CAP
     for j in range(2):
 
@@ -208,15 +208,20 @@
             v = px[k // 4]
             k = k % 4
             return v[96 * j : 96 * j + 96, 256 * k : 256 * k + 256]
+
+        def store(v, lo, hi):
+            for z in range(NZ):
+                at = 64 * z + 32 * j
+                back[at : at + 32, lo:hi] = v[32 * z : 32 * z + 32]
 
         lo, hi = piece(6), piece(7)
         ends = ((c60, lo, c71, hi), (c60, hi, c72, lo), (c61, lo, c72, hi))
         for n in range(3):
             a, va, b, vb = ends[n]
             v = dot(first, piece(n)) + dot(second, piece(n + 3)) + dot(a, va) + dot(b, vb)
-            back[256 * j : 256 * j + 256, 256 * n : 256 * n + 256] = v.astype(bf16)
+            store(v.astype(bf16), 256 * n, 256 * n + 256)
         last = dot(for_dot, dots[96 * j : 96 * j + 96, :]) + jnp.where(count_at, tally, 0.0)
-        back[256 * j : 256 * j + 256, 768:BACK] = last.astype(bf16)
+        store(last.astype(bf16), 768, BACK)
 
 
 def weight_grads(x_rows, g_rows, grads, keep, send):
@@ -244,10 +249,13 @@
     s0[...] = total(0)
 
 
-def join(s2, right, s4, s6, left, t2, t6):
-    far = slice(0, 3 * BLK)
-    t2[...] = (s2[...].astype(f32) + right[far].astype(f32) + s4[...].astype(f32)).astype(bf16)
-    t6[...] = (s6[...].astype(f32) + left[far].astype(f32)).astype(bf16)
+def join_right(s2, right, s4, t2):
+    near = right[0 : 3 * BLK].astype(f32)
+    t2[...] = (s2[...].astype(f32) + near + s4[...].astype(f32)).astype(bf16)
+
+
+def join_left(s6, left, t6):
+    t6[...] = (s6[...].astype(f32) + left[0 : 3 * BLK].astype(f32)).astype(bf16)
 
 
 def sum_chips(s0, right, left, t2, t6, gate, up, down):
@@ -308,30 +316,35 @@
 def body(tokens, cotangent, routes, logits, w_gate, w_up, w_down):
     routes_t = routes.T
     shard = call(pack_weights, shape(SHARD, HID), 4, limit=60)(routes_t, w_gate, w_up, w_down)
+    rows = call(send_rows, shape(NZ, 8, DM), 4, limit=60)(tokens, cotangent, routes_t, logits)
+    rows = exchange(rows, "z")
+    rows = call(repack, shape(NY, 48, DM), 1)(rows.reshape(8 * NZ, DM))
+    came = exchange(rows, "y")
     p2 = shifted(shard, 2)
     m2 = shifted(shard, 6)
-    wire = call(send_rows, shape(NSRC, 8, WIRE), 4, limit=60)(tokens, cotangent, routes_t, logits)
-    came = exchange(wire, ("z", "y"))
     p1 = shifted(shard, 1)
-    m1 = shifted(shard, 7)
     p4 = shifted(p2, 2)
     p3 = shifted(p2, 1)
     m3 = shifted(m2, 7)
-    own = call(stack_shards, shape(8, SHARD, HID), 8)(shard, p1, p2, p3, p4, m3, m2, m1)
+    m1 = shifted(shard, 7)
+    own = call(
+        stack_shards,
+        shape(8, SHARD, HID),
+        8,
+        far=HELD,
+        scratch=(pltpu.SemaphoreType.DMA((len(HELD),)),),
+    )(
+        shard, p1, p2, p3, p4, m3, m2, m1
+    )
     oth = lax.ppermute(own, "c", SWAP)
-    x_rows, g_rows, grads, dots, oth = call(
+    x_rows, g_rows = call(unpack, (shape(ROWS, DM), shape(ROWS, DM)), 1)(came.reshape(48 * NY, DM))
+    grads, dots, oth = call(
         forward,
-        (
-            shape(ROWS, DM),
-            shape(ROWS, DM),
-            shape(ROWS, 3 * HID),
-            shape(ROWS, BLK),
-            shape(8, SHARD, HID),
-        ),
-        3,
-        far=(2,),
+        (shape(ROWS, 3 * HID), shape(ROWS, BLK), shape(8, SHARD, HID)),
+        4,
+        far=(3,),
         scratch=(pltpu.SemaphoreType.DMA,),
-    )(came.reshape(8 * NSRC, WIRE), own, oth)
+    )(x_rows, g_rows, own, oth)
     keep, send = call(
         weight_grads, (shape(8, 3 * BLK, HID), shape(8, 3 * BLK, HID)), 3
     )(x_rows, g_rows, grads)
@@ -339,12 +352,14 @@
     back = call(row_grads, shape(8 * NSRC, BACK), 4)(grads, dots, own, oth)
     one, two = shape(3 * BLK, HID), shape(6 * BLK, HID)
     s0, s2, s4, s6, right, left = call(add_cores, (one, one, one, one, two, two), 2)(keep, other)
-    right = shifted(right, 1)
     s4 = shifted(s4, 2)
     left = shifted(left, 7)
     back = exchange(back.reshape(NSRC, 8, BACK), ("z", "y"))
-    t2, t6 = call(join, (one, one), 5)(s2, right, s4, s6, left)
-    t2, t6 = shifted(t2, 2), shifted(t6, 6)
+    right = shifted(right, 1)
+    t6 = call(join_left, one, 2)(s6, left)
+    t6 = shifted(t6, 6)
+    t2 = call(join_right, one, 3)(s2, right, s4)
+    t2 = shifted(t2, 2)
     grad_gate, grad_up, grad_down = call(
         sum_chips, (shape(BLK, HID), shape(BLK, HID), shape(HID, BLK)), 5
     )(s0, right, left, t2, t6)

time: 138 us -> 145 us (1.051)
  blocking collectives: 0 us -> 28.6 us
  starting transfers between devices: 85.7 us -> 68.7 us
  waiting for transfers between devices: 32.3 us -> 28.3 us
  local copies, waits for them, and re-layouts: 3.57 us -> 0.94 us
  Pallas kernels: 14.9 us -> 16.4 us
    all_to_all x0 -> x1, blocking collectives: none -> 28.6 us  [exchange(): return lax.all_to_all(value, axis, split_axis=0, concat_axis=0, tiled=True)]
    all_to_all x2, starting transfers between devices: 35.8 us -> 17.3 us  [exchange(): return lax.all_to_all(value, axis, split_axis=0, concat_axis=0, tiled=True)]
    ppermute x12, waiting for transfers between devices: 28.8 us -> 24.9 us  [shifted(): return lax.ppermute(value, 'x', [(i, (i + by) % NX) for i in range(NX)])]
    unnamed x10 -> x6, local copies, waits for them, and re-layouts: 3.57 us -> 0.94 us
    ppermute x12, starting transfers between devices: 45.9 us -> 47.5 us  [shifted(): return lax.ppermute(value, 'x', [(i, (i + by) % NX) for i in range(NX)])]
    pallas_call x4 -> x7, Pallas kernels: 5.13 us -> 6.54 us  [the longest x1 2.3 us: body(): call(forward, (shape(ROWS, 3 * HID), shape(ROWS, BLK), shape(8, SHARD, HI...]
where the time goes in v2:
time: 145 us; the launch traced here: 144 us
  starting transfers between devices  68.7 us (47%)
  blocking collectives  28.6 us (20%)
  waiting for transfers between devices  28.3 us (20%)
  Pallas kernels  16.4 us (11%)
    ppermute x12, starting transfers between devices, shifted(): return lax.ppermute(value, 'x', [(i, (i + by) % NX) for i in range(NX)])  47.5 us
    all_to_all x1, blocking collectives, exchange(): return lax.all_to_all(value, axis, split_axis=0, concat_axis=0, tiled=True)  28.6 us
    ppermute x12, waiting for transfers between devices, shifted(): return lax.ppermute(value, 'x', [(i, (i + by) % NX) for i in range(NX)])  24.9 us
    all_to_all x2, starting transfers between devices, exchange(): return lax.all_to_all(value, axis, split_axis=0, concat_axis=0, tiled=True)  17.3 us
  transfers between devices with their start and end apart: 16, of which 7 were waited for; matrix products, arithmetic and copies ran while one was open for 0% of the time, Pallas kernels for 5%

profile of v2, /device:TPU:4, one launch (start us, length us, event | category | flops | bytes accessed | tf_op | source)
XLA Modules:
  0.0 143.7 jit_solution(9059413923976616456)
XLA Ops:
  0.6 2.0 %shard_map.118 = bf16[8,8,2048]{2,1,0:T(8,128)(2,1)} custom-call(bf16[8,2048]{1,0:T(8,128)(2,1)} %tokens.1, bf16[8,2048]{1,0:T(8,128)(2,1)} %cotangent.1, s32[2,8]{1,0:T(2,128)} %bitcast.9, f32[8,8]{1,0:T(8,128)} %logits.3), custom_call_target="tpu_custom_call" | custom-call | tf_op jit(solution)/shard_map/pallas_call | solution.py:319
  2.6 28.6 %all_to_all.15 = bf16[8,8,2048]{2,1,0:T(8,128)(2,1)S(1)} all-to-all(bf16[8,8,2048]{2,1,0:T(8,128)(2,1)} %shard_map.118), channel_id=1, replica_groups=mesh['x'=8,'c'=2,'z'=8,'y'=8] {'z'}, dimensions={0} | all-to-all | bytes 524288 | tf_op jit(solution)/shard_map/all_to_all | solution.py:313
  31.2 1.4 shard_map.119
  32.6 7.6 %all-to-all-start.1 = ((bf16[8,48,2048]{2,1,0:T(8,128)(2,1)}), bf16[8,48,2048]{2,1,0:T(8,128)(2,1)S(1)}, u32[]{:S(2)}, u32[]{:S(2)}) async-start(bf16[8,48,2048]{2,1,0:T(8,128)(2,1)} %shard_map.119), calls=%async_computation.1 | async-start | bytes 3145728 | tf_op jit(solution)/shard_map/all_to_all | solution.py:313
  40.2 1.7 %shard_map.121.refs_0_ = bf16[392,256]{1,0:T(8,128)(2,1)} custom-call(s32[2,8]{1,0:T(2,128)} %bitcast.10, bf16[128,256]{1,0:T(8,128)(2,1)} %w_gate.1, bf16[128,256]{1,0:T(8,128)(2,1)} %w_up.1, bf16[256,128]{1,0:T(8,128)(2,1)} %w_down.1), custom_call_target="tpu_custom_call" | custom-call | tf_op jit(solution)/shard_map/pallas_call | solution.py:318
  41.9 2.4 %collective-permute-start.4 = (bf16[392,256]{1,0:T(8,128)(2,1)}, bf16[392,256]{1,0:T(8,128)(2,1)S(1)}, u32[]{:S(2)}, u32[]{:S(2)}) collective-permute-start(bf16[392,256]{1,0:T(8,128)(2,1)} %shard_map.121.refs_0_), channel_id=1, source_target_pairs={{0,768},{128,896},{256,0},{384,128},{512,256},{640,384},{768,512},... | collective-permute-start | bytes 602120 | tf_op jit(solution)/shard_map/ppermute | solution.py:309
  44.3 5.5 %collective-permute-start.1 = (bf16[392,256]{1,0:T(8,128)(2,1)}, bf16[392,256]{1,0:T(8,128)(2,1)S(1)}, u32[]{:S(2)}, u32[]{:S(2)}) collective-permute-start(bf16[392,256]{1,0:T(8,128)(2,1)} %shard_map.121.refs_0_), channel_id=1, source_target_pairs={{0,256},{128,384},{256,512},{384,640},{512,768},{640,896},{768,0},... | collective-permute-start | bytes 602120 | tf_op jit(solution)/shard_map/ppermute | solution.py:309
  49.8 1.9 %collective-permute-start.6 = (bf16[392,256]{1,0:T(8,128)(2,1)}, bf16[392,256]{1,0:T(8,128)(2,1)S(1)}, u32[]{:S(2)}, u32[]{:S(2)}) collective-permute-start(bf16[392,256]{1,0:T(8,128)(2,1)} %shard_map.121.refs_0_), channel_id=1, source_target_pairs={{0,896},{128,0},{256,128},{384,256},{512,384},{640,512},{768,640},... | collective-permute-start | bytes 602120 | tf_op jit(solution)/shard_map/ppermute | solution.py:309
  51.8 3.9 %collective-permute-start = (bf16[392,256]{1,0:T(8,128)(2,1)}, bf16[392,256]{1,0:T(8,128)(2,1)S(1)}, u32[]{:S(2)}, u32[]{:S(2)}) collective-permute-start(bf16[392,256]{1,0:T(8,128)(2,1)} %shard_map.121.refs_0_), channel_id=1, source_target_pairs={{0,128},{128,256},{256,384},{384,512},{512,640},{640,768},{768,896... | collective-permute-start | bytes 602120 | tf_op jit(solution)/shard_map/ppermute | solution.py:309
  55.7 1.9 %collective-permute-start.5 = (bf16[392,256]{1,0:T(8,128)(2,1)S(1)}, bf16[392,256]{1,0:T(8,128)(2,1)S(1)}, u32[]{:S(2)}, u32[]{:S(2)}) collective-permute-start(bf16[392,256]{1,0:T(8,128)(2,1)S(1)} %collective-permute-done.4.refs_6_), channel_id=1, source_target_pairs={{0,896},{128,0},{256,128},{384,256},{512,384},{640,512},{768,640},... | collective-permute-start | bytes 602120 | tf_op jit(solution)/shard_map/ppermute | solution.py:309
  57.6 7.3 %collective-permute-start.3 = (bf16[392,256]{1,0:T(8,128)(2,1)S(1)}, bf16[392,256]{1,0:T(8,128)(2,1)S(1)}, u32[]{:S(2)}, u32[]{:S(2)}) collective-permute-start(bf16[392,256]{1,0:T(8,128)(2,1)S(1)} %collective-permute-done.1.refs_2_), channel_id=1, source_target_pairs={{0,256},{128,384},{256,512},{384,640},{512,768},{640,896},{768,0},... | collective-permute-start | bytes 602120 | tf_op jit(solution)/shard_map/ppermute | solution.py:309
  64.9 2.5 %collective-permute-start.2 = (bf16[392,256]{1,0:T(8,128)(2,1)S(1)}, bf16[392,256]{1,0:T(8,128)(2,1)S(1)}, u32[]{:S(2)}, u32[]{:S(2)}) collective-permute-start(bf16[392,256]{1,0:T(8,128)(2,1)S(1)} %collective-permute-done.1.refs_2_), channel_id=1, source_target_pairs={{0,128},{128,256},{256,384},{384,512},{512,640},{640,768},{768,896... | collective-permute-start | bytes 602120 | tf_op jit(solution)/shard_map/ppermute | solution.py:309
  67.5 4.8 %collective-permute-done.3.refs_4_ = bf16[392,256]{1,0:T(8,128)(2,1)S(1)} collective-permute-done((bf16[392,256]{1,0:T(8,128)(2,1)S(1)}, bf16[392,256]{1,0:T(8,128)(2,1)S(1)}, u32[]{:S(2)}, u32[]{:S(2)}) %collective-permute-start.3) | collective-permute-done | bytes 200736 | tf_op jit(solution)/shard_map/ppermute | solution.py:309
  72.3 1.6 %collective-permute-done.2.refs_3_ = bf16[392,256]{1,0:T(8,128)(2,1)S(1)} collective-permute-done((bf16[392,256]{1,0:T(8,128)(2,1)S(1)}, bf16[392,256]{1,0:T(8,128)(2,1)S(1)}, u32[]{:S(2)}, u32[]{:S(2)}) %collective-permute-start.2) | collective-permute-done | bytes 200736 | tf_op jit(solution)/shard_map/ppermute | solution.py:309
  75.4 1.9 %collective-permute-start.7 = (bf16[8,392,256]{2,1,0:T(8,128)(2,1)S(1)}, bf16[8,392,256]{2,1,0:T(8,128)(2,1)}, u32[]{:S(2)}, u32[]{:S(2)}) collective-permute-start(bf16[8,392,256]{2,1,0:T(8,128)(2,1)S(1)} %shard_map.122.own), channel_id=1, source_target_pairs={{0,64},{64,0},{1,65},{65,1},{2,66},{66,2},{3,67},{67,3},{4,68},{68... | collective-permute-start | bytes 4816904 | tf_op jit(solution)/shard_map/ppermute | solution.py:339
  77.4 1.1 all-to-all-done.1
  78.6 2.4 %collective-permute-done.7.far = bf16[8,392,256]{2,1,0:T(8,128)(2,1)} collective-permute-done((bf16[8,392,256]{2,1,0:T(8,128)(2,1)S(1)}, bf16[8,392,256]{2,1,0:T(8,128)(2,1)}, u32[]{:S(2)}, u32[]{:S(2)}) %collective-permute-start.7) | collective-permute-done | bytes 1605664 | tf_op jit(solution)/shard_map/ppermute | solution.py:339
  80.9 2.3 %shard_map.123 = (bf16[192,768]{1,0:T(8,128)(2,1)S(1)}, bf16[192,128]{1,0:T(8,128)(2,1)S(1)}, bf16[8,392,256]{2,1,0:T(8,128)(2,1)S(1)}) custom-call(bf16[192,2048]{1,0:T(8,128)(2,1)S(1)} %get-tuple-element.25.x_rows, bf16[192,2048]{1,0:T(8,128)(2,1)S(1)} %get-tuple-element.26.g_rows, bf16[8,392,256]{2,1,0:T(8,128)(2,1)S(1)} %shard_map.122.own, ...), custom_call_target="tpu_custom_call" | custom-call | tf_op jit(solution)/shard_map/pallas_call | solution.py:341
  83.2 2.0 %shard_map.126 = (bf16[8,384,256]{2,1,0:T(8,128)(2,1)S(1)}, bf16[8,384,256]{2,1,0:T(8,128)(2,1)}) custom-call(bf16[192,2048]{1,0:T(8,128)(2,1)S(1)} %get-tuple-element.25.x_rows, bf16[192,2048]{1,0:T(8,128)(2,1)S(1)} %get-tuple-element.26.g_rows, bf16[192,768]{1,0:T(8,128)(2,1)S(1)} %get-tuple-element.27.grads), custom_call_target="tpu_custom_call" | custom-call | tf_op jit(solution)/shard_map/pallas_call | solution.py:348
  85.2 2.0 %collective-permute-start.8 = (bf16[8,384,256]{2,1,0:T(8,128)(2,1)}, bf16[8,384,256]{2,1,0:T(8,128)(2,1)}, u32[]{:S(2)}, u32[]{:S(2)}) collective-permute-start(bf16[8,384,256]{2,1,0:T(8,128)(2,1)} %get-tuple-element.34), channel_id=1, source_target_pairs={{0,64},{64,0},{1,65},{65,1},{2,66},{66,2},{3,67},{67,3},{4,68},{68... | collective-permute-start | bytes 4718600 | tf_op jit(solution)/shard_map/ppermute | solution.py:351
  87.2 2.7 %shard_map.124 = bf16[512,896]{1,0:T(8,128)(2,1)} custom-call(bf16[192,768]{1,0:T(8,128)(2,1)S(1)} %get-tuple-element.27.grads, bf16[192,128]{1,0:T(8,128)(2,1)S(1)} %get-tuple-element.28.dots, bf16[8,392,256]{2,1,0:T(8,128)(2,1)S(1)} %shard_map.122.own, bf16[8,392,256]{2,1,0:T(8,128)(2,1)S(1)} %get-tuple-element.29.oth), custom_call_target="tpu_custom_call" | custom-call | tf_op jit(solution)/shard_map/pallas_call | solution.py:352
  89.9 9.7 %all-to-all-start.2 = ((bf16[64,8,896]{2,1,0:T(8,128)(2,1)}), bf16[64,8,896]{2,1,0:T(8,128)(2,1)S(1)}, u32[]{:S(2)}, u32[]{:S(2)}) async-start(bf16[64,8,896]{2,1,0:T(8,128)(2,1)} %bitcast.3), calls=%async_computation.2 | async-start | bytes 1835008 | tf_op jit(solution)/shard_map/all_to_all | solution.py:313
  99.6 1.8 %shard_map.127 = (bf16[384,256]{1,0:T(8,128)(2,1)S(1)}, bf16[384,256]{1,0:T(8,128)(2,1)S(1)}, bf16[384,256]{1,0:T(8,128)(2,1)S(1)}, bf16[384,256]{1,0:T(8,128)(2...) custom-call(bf16[8,384,256]{2,1,0:T(8,128)(2,1)S(1)} %get-tuple-element.33.keep, ...), custom_call_target="tpu_custom_call" | custom-call | tf_op jit(solution)/shard_map/pallas_call | solution.py:354
  101.4 3.8 %collective-permute-start.9 = (bf16[768,256]{1,0:T(8,128)(2,1)S(1)}, bf16[768,256]{1,0:T(8,128)(2,1)S(1)}, u32[]{:S(2)}, u32[]{:S(2)}) collective-permute-start(bf16[768,256]{1,0:T(8,128)(2,1)S(1)} %get-tuple-element.36), channel_id=1, source_target_pairs={{0,128},{128,256},{256,384},{384,512},{512,640},{640,768},{768,896... | collective-permute-start | bytes 1179656 | tf_op jit(solution)/shard_map/ppermute | solution.py:309
  105.3 2.0 %collective-permute-start.10 = (bf16[768,256]{1,0:T(8,128)(2,1)S(1)}, bf16[768,256]{1,0:T(8,128)(2,1)S(1)}, u32[]{:S(2)}, u32[]{:S(2)}) collective-permute-start(bf16[768,256]{1,0:T(8,128)(2,1)S(1)} %get-tuple-element.37), channel_id=1, source_target_pairs={{0,896},{128,0},{256,128},{384,256},{512,384},{640,512},{768,640},... | collective-permute-start | bytes 1179656 | tf_op jit(solution)/shard_map/ppermute | solution.py:309
  107.3 7.6 %collective-permute-start.11 = (bf16[384,256]{1,0:T(8,128)(2,1)S(1)}, bf16[384,256]{1,0:T(8,128)(2,1)S(1)}, u32[]{:S(2)}, u32[]{:S(2)}) collective-permute-start(bf16[384,256]{1,0:T(8,128)(2,1)S(1)} %get-tuple-element.39), channel_id=1, source_target_pairs={{0,256},{128,384},{256,512},{384,640},{512,768},{640,896},{768,0},... | collective-permute-start | bytes 589832 | tf_op jit(solution)/shard_map/ppermute | solution.py:309
  114.9 7.4 %collective-permute-done.11.s4 = bf16[384,256]{1,0:T(8,128)(2,1)S(1)} collective-permute-done((bf16[384,256]{1,0:T(8,128)(2,1)S(1)}, bf16[384,256]{1,0:T(8,128)(2,1)S(1)}, u32[]{:S(2)}, u32[]{:S(2)}) %collective-permute-start.11) | collective-permute-done | bytes 196640 | tf_op jit(solution)/shard_map/ppermute | solution.py:309
  122.4 6.6 %collective-permute-start.12 = (bf16[384,256]{1,0:T(8,128)(2,1)S(1)}, bf16[384,256]{1,0:T(8,128)(2,1)S(1)}, u32[]{:S(2)}, u32[]{:S(2)}) collective-permute-start(bf16[384,256]{1,0:T(8,128)(2,1)S(1)} %shard_map.128), channel_id=1, source_target_pairs={{0,256},{128,384},{256,512},{384,640},{512,768},{640,896},{768,0},... | collective-permute-start | bytes 589832 | tf_op jit(solution)/shard_map/ppermute | solution.py:309
  129.1 1.9 %collective-permute-start.13 = (bf16[384,256]{1,0:T(8,128)(2,1)S(1)}, bf16[384,256]{1,0:T(8,128)(2,1)S(1)}, u32[]{:S(2)}, u32[]{:S(2)}) collective-permute-start(bf16[384,256]{1,0:T(8,128)(2,1)S(1)} %shard_map.129), channel_id=1, source_target_pairs={{0,768},{128,896},{256,0},{384,128},{512,256},{640,384},{768,512},... | collective-permute-start | bytes 589832 | tf_op jit(solution)/shard_map/ppermute | solution.py:309
  131.0 0.9 shard_map.125
  132.0 4.2 %collective-permute-done.12.t2 = bf16[384,256]{1,0:T(8,128)(2,1)S(1)} collective-permute-done((bf16[384,256]{1,0:T(8,128)(2,1)S(1)}, bf16[384,256]{1,0:T(8,128)(2,1)S(1)}, u32[]{:S(2)}, u32[]{:S(2)}) %collective-permute-start.12) | collective-permute-done | bytes 196640 | tf_op jit(solution)/shard_map/ppermute | solution.py:309
  136.2 6.8 %collective-permute-done.13.t6 = bf16[384,256]{1,0:T(8,128)(2,1)S(1)} collective-permute-done((bf16[384,256]{1,0:T(8,128)(2,1)S(1)}, bf16[384,256]{1,0:T(8,128)(2,1)S(1)}, u32[]{:S(2)}, u32[]{:S(2)}) %collective-permute-start.13) | collective-permute-done | bytes 196640 | tf_op jit(solution)/shard_map/ppermute | solution.py:309
  (20 shorter events, 2.6 us)
Async XLA Ops:
  32.6 45.8 %all-to-all-start.1 = ((bf16[8,48,2048]{2,1,0:T(8,128)(2,1)}), bf16[8,48,2048]{2,1,0:T(8,128)(2,1)S(1)}, u32[]{:S(2)}, u32[]{:S(2)}) async-start(bf16[8,48,2048]{2,1,0:T(8,128)(2,1)} %shard_map.119), calls=%async_computation.1 | async-start | bytes 3145728 | tf_op jit(solution)/shard_map/all_to_all | solution.py:313
  41.9 13.8 %collective-permute-start.4 = (bf16[392,256]{1,0:T(8,128)(2,1)}, bf16[392,256]{1,0:T(8,128)(2,1)S(1)}, u32[]{:S(2)}, u32[]{:S(2)}) collective-permute-start(bf16[392,256]{1,0:T(8,128)(2,1)} %shard_map.121.refs_0_), channel_id=1, source_target_pairs={{0,768},{128,896},{256,0},{384,128},{512,256},{640,384},{768,512},... | collective-permute-start | bytes 602120 | tf_op jit(solution)/shard_map/ppermute | solution.py:309
  44.3 13.3 %collective-permute-start.1 = (bf16[392,256]{1,0:T(8,128)(2,1)}, bf16[392,256]{1,0:T(8,128)(2,1)S(1)}, u32[]{:S(2)}, u32[]{:S(2)}) collective-permute-start(bf16[392,256]{1,0:T(8,128)(2,1)} %shard_map.121.refs_0_), channel_id=1, source_target_pairs={{0,256},{128,384},{256,512},{384,640},{512,768},{640,896},{768,0},... | collective-permute-start | bytes 602120 | tf_op jit(solution)/shard_map/ppermute | solution.py:309
  49.8 17.6 %collective-permute-start.6 = (bf16[392,256]{1,0:T(8,128)(2,1)}, bf16[392,256]{1,0:T(8,128)(2,1)S(1)}, u32[]{:S(2)}, u32[]{:S(2)}) collective-permute-start(bf16[392,256]{1,0:T(8,128)(2,1)} %shard_map.121.refs_0_), channel_id=1, source_target_pairs={{0,896},{128,0},{256,128},{384,256},{512,384},{640,512},{768,640},... | collective-permute-start | bytes 602120 | tf_op jit(solution)/shard_map/ppermute | solution.py:309
  51.8 15.7 %collective-permute-start = (bf16[392,256]{1,0:T(8,128)(2,1)}, bf16[392,256]{1,0:T(8,128)(2,1)S(1)}, u32[]{:S(2)}, u32[]{:S(2)}) collective-permute-start(bf16[392,256]{1,0:T(8,128)(2,1)} %shard_map.121.refs_0_), channel_id=1, source_target_pairs={{0,128},{128,256},{256,384},{384,512},{512,640},{640,768},{768,896... | collective-permute-start | bytes 602120 | tf_op jit(solution)/shard_map/ppermute | solution.py:309
  55.7 11.8 %collective-permute-start.5 = (bf16[392,256]{1,0:T(8,128)(2,1)S(1)}, bf16[392,256]{1,0:T(8,128)(2,1)S(1)}, u32[]{:S(2)}, u32[]{:S(2)}) collective-permute-start(bf16[392,256]{1,0:T(8,128)(2,1)S(1)} %collective-permute-done.4.refs_6_), channel_id=1, source_target_pairs={{0,896},{128,0},{256,128},{384,256},{512,384},{640,512},{768,640},... | collective-permute-start | bytes 602120 | tf_op jit(solution)/shard_map/ppermute | solution.py:309
  57.6 14.7 %collective-permute-start.3 = (bf16[392,256]{1,0:T(8,128)(2,1)S(1)}, bf16[392,256]{1,0:T(8,128)(2,1)S(1)}, u32[]{:S(2)}, u32[]{:S(2)}) collective-permute-start(bf16[392,256]{1,0:T(8,128)(2,1)S(1)} %collective-permute-done.1.refs_2_), channel_id=1, source_target_pairs={{0,256},{128,384},{256,512},{384,640},{512,768},{640,896},{768,0},... | collective-permute-start | bytes 602120 | tf_op jit(solution)/shard_map/ppermute | solution.py:309
  64.9 9.0 %collective-permute-start.2 = (bf16[392,256]{1,0:T(8,128)(2,1)S(1)}, bf16[392,256]{1,0:T(8,128)(2,1)S(1)}, u32[]{:S(2)}, u32[]{:S(2)}) collective-permute-start(bf16[392,256]{1,0:T(8,128)(2,1)S(1)} %collective-permute-done.1.refs_2_), channel_id=1, source_target_pairs={{0,128},{128,256},{256,384},{384,512},{512,640},{640,768},{768,896... | collective-permute-start | bytes 602120 | tf_op jit(solution)/shard_map/ppermute | solution.py:309
  73.9 0.9 copy-start
  75.4 5.5 %collective-permute-start.7 = (bf16[8,392,256]{2,1,0:T(8,128)(2,1)S(1)}, bf16[8,392,256]{2,1,0:T(8,128)(2,1)}, u32[]{:S(2)}, u32[]{:S(2)}) collective-permute-start(bf16[8,392,256]{2,1,0:T(8,128)(2,1)S(1)} %shard_map.122.own), channel_id=1, source_target_pairs={{0,64},{64,0},{1,65},{65,1},{2,66},{66,2},{3,67},{67,3},{4,68},{68... | collective-permute-start | bytes 4816904 | tf_op jit(solution)/shard_map/ppermute | solution.py:339
  85.2 14.4 %collective-permute-start.8 = (bf16[8,384,256]{2,1,0:T(8,128)(2,1)}, bf16[8,384,256]{2,1,0:T(8,128)(2,1)}, u32[]{:S(2)}, u32[]{:S(2)}) collective-permute-start(bf16[8,384,256]{2,1,0:T(8,128)(2,1)} %get-tuple-element.34), channel_id=1, source_target_pairs={{0,64},{64,0},{1,65},{65,1},{2,66},{66,2},{3,67},{67,3},{4,68},{68... | collective-permute-start | bytes 4718600 | tf_op jit(solution)/shard_map/ppermute | solution.py:351
  89.9 41.1 %all-to-all-start.2 = ((bf16[64,8,896]{2,1,0:T(8,128)(2,1)}), bf16[64,8,896]{2,1,0:T(8,128)(2,1)S(1)}, u32[]{:S(2)}, u32[]{:S(2)}) async-start(bf16[64,8,896]{2,1,0:T(8,128)(2,1)} %bitcast.3), calls=%async_computation.2 | async-start | bytes 1835008 | tf_op jit(solution)/shard_map/all_to_all | solution.py:313
  101.4 29.6 %copy-start.1 = (f32[8,8]{1,0:T(8,128)S(1)}, f32[8,8]{1,0:T(8,128)}, u32[]{:S(2)}) copy-start(f32[8,8]{1,0:T(8,128)} %logits.3) | copy-start | bytes 772
  101.4 29.6 %copy-start.2 = (s32[8,2]{0,1:T(2,128)S(1)}, s32[8,2]{0,1:T(2,128)}, u32[]{:S(2)}) copy-start(s32[8,2]{0,1:T(2,128)} %param.9) | copy-start | bytes 196
  101.4 20.9 %collective-permute-start.9 = (bf16[768,256]{1,0:T(8,128)(2,1)S(1)}, bf16[768,256]{1,0:T(8,128)(2,1)S(1)}, u32[]{:S(2)}, u32[]{:S(2)}) collective-permute-start(bf16[768,256]{1,0:T(8,128)(2,1)S(1)} %get-tuple-element.36), channel_id=1, source_target_pairs={{0,128},{128,256},{256,384},{384,512},{512,640},{640,768},{768,896... | collective-permute-start | bytes 1179656 | tf_op jit(solution)/shard_map/ppermute | solution.py:309
  105.3 23.7 %collective-permute-start.10 = (bf16[768,256]{1,0:T(8,128)(2,1)S(1)}, bf16[768,256]{1,0:T(8,128)(2,1)S(1)}, u32[]{:S(2)}, u32[]{:S(2)}) collective-permute-start(bf16[768,256]{1,0:T(8,128)(2,1)S(1)} %get-tuple-element.37), channel_id=1, source_target_pairs={{0,896},{128,0},{256,128},{384,256},{512,384},{640,512},{768,640},... | collective-permute-start | bytes 1179656 | tf_op jit(solution)/shard_map/ppermute | solution.py:309
  107.3 15.0 %collective-permute-start.11 = (bf16[384,256]{1,0:T(8,128)(2,1)S(1)}, bf16[384,256]{1,0:T(8,128)(2,1)S(1)}, u32[]{:S(2)}, u32[]{:S(2)}) collective-permute-start(bf16[384,256]{1,0:T(8,128)(2,1)S(1)} %get-tuple-element.39), channel_id=1, source_target_pairs={{0,256},{128,384},{256,512},{384,640},{512,768},{640,896},{768,0},... | collective-permute-start | bytes 589832 | tf_op jit(solution)/shard_map/ppermute | solution.py:309
  122.4 13.8 %collective-permute-start.12 = (bf16[384,256]{1,0:T(8,128)(2,1)S(1)}, bf16[384,256]{1,0:T(8,128)(2,1)S(1)}, u32[]{:S(2)}, u32[]{:S(2)}) collective-permute-start(bf16[384,256]{1,0:T(8,128)(2,1)S(1)} %shard_map.128), channel_id=1, source_target_pairs={{0,256},{128,384},{256,512},{384,640},{512,768},{640,896},{768,0},... | collective-permute-start | bytes 589832 | tf_op jit(solution)/shard_map/ppermute | solution.py:309
  129.1 13.9 %collective-permute-start.13 = (bf16[384,256]{1,0:T(8,128)(2,1)S(1)}, bf16[384,256]{1,0:T(8,128)(2,1)S(1)}, u32[]{:S(2)}, u32[]{:S(2)}) collective-permute-start(bf16[384,256]{1,0:T(8,128)(2,1)S(1)} %shard_map.129), channel_id=1, source_target_pairs={{0,768},{128,896},{256,0},{384,128},{512,256},{640,384},{768,512},... | collective-permute-start | bytes 589832 | tf_op jit(solution)/shard_map/ppermute | solution.py:309

commit v3 on v1

--- a/solution.py
+++ b/solution.py
@@ -144,9 +144,7 @@
     return ref[:, k * BLK : (k + 1) * BLK, :].reshape(DM // 2, HID)
 
 
-def forward(wire, own, far, x_out, g_out, grads_out, dots_out, oth, sem):
-    fetch = pltpu.make_async_copy(far, oth, sem)
-    fetch.start()
+def unpack(wire, x_out, g_out):
     to, fr = iota((192, 256), 0), iota((192, 256), 1)
     main = one_hot(fr == 8 * (to & 31) + (to >> 5))
     to, fr = iota((64, 256), 0), iota((64, 256), 1)
@@ -160,12 +158,17 @@
             tail = dot(ends, wire[256 * j : 256 * j + 256, 512 * r : 512 * r + 512]).astype(bf16)
             x_out[at : at + 32, WIRE:DM] = tail[0:32]
             g_out[at : at + 32, WIRE:DM] = tail[32:64]
+
+
+def forward(x_rows, g_rows, own, far, grads_out, dots_out, oth, sem):
+    fetch = pltpu.make_async_copy(far, oth, sem)
+    fetch.start()
     half = DM // 2
-    near = [dot(rows[:, 0:half], weight(own, k)) for k, rows in enumerate((x_out, x_out, g_out))]
+    near = [dot(rows[:, 0:half], weight(own, k)) for k, rows in enumerate((x_rows, x_rows, g_rows))]
     fetch.wait()
     gate_pre, up_pre, hidden_grad = [
         near[k] + dot(rows[:, half:DM], weight(oth, k))
-        for k, rows in enumerate((x_out, x_out, g_out))
+        for k, rows in enumerate((x_rows, x_rows, g_rows))
     ]
     sigma = 1.0 / (1.0 + jnp.exp(-gate_pre))
     active = gate_pre * sigma
@@ -244,10 +247,13 @@
     s0[...] = total(0)
 
 
-def join(s2, right, s4, s6, left, t2, t6):
-    far = slice(0, 3 * BLK)
-    t2[...] = (s2[...].astype(f32) + right[far].astype(f32) + s4[...].astype(f32)).astype(bf16)
-    t6[...] = (s6[...].astype(f32) + left[far].astype(f32)).astype(bf16)
+def join_right(s2, right, s4, t2):
+    near = right[0 : 3 * BLK].astype(f32)
+    t2[...] = (s2[...].astype(f32) + near + s4[...].astype(f32)).astype(bf16)
+
+
+def join_left(s6, left, t6):
+    t6[...] = (s6[...].astype(f32) + left[0 : 3 * BLK].astype(f32)).astype(bf16)
 
 
 def sum_chips(s0, right, left, t2, t6, gate, up, down):
@@ -307,7 +313,7 @@
 
 def body(tokens, cotangent, routes, logits, w_gate, w_up, w_down):
     routes_t = routes.T
-    shard = call(pack_weights, shape(SHARD, HID), 4, limit=60)(routes_t, w_gate, w_up, w_down)
+    shard = call(pack_weights, shape(SHARD, HID), 4)(routes_t, w_gate, w_up, w_down)
     p2 = shifted(shard, 2)
     m2 = shifted(shard, 6)
     wire = call(send_rows, shape(NSRC, 8, WIRE), 4, limit=60)(tokens, cotangent, routes_t, logits)
@@ -319,19 +325,16 @@
     m3 = shifted(m2, 7)
     own = call(stack_shards, shape(8, SHARD, HID), 8)(shard, p1, p2, p3, p4, m3, m2, m1)
     oth = lax.ppermute(own, "c", SWAP)
-    x_rows, g_rows, grads, dots, oth = call(
+    x_rows, g_rows = call(unpack, (shape(ROWS, DM), shape(ROWS, DM)), 1)(
+        came.reshape(8 * NSRC, WIRE)
+    )
+    grads, dots, oth = call(
         forward,
-        (
-            shape(ROWS, DM),
-            shape(ROWS, DM),
-            shape(ROWS, 3 * HID),
-            shape(ROWS, BLK),
-            shape(8, SHARD, HID),
-        ),
-        3,
-        far=(2,),
+        (shape(ROWS, 3 * HID), shape(ROWS, BLK), shape(8, SHARD, HID)),
+        4,
+        far=(3,),
         scratch=(pltpu.SemaphoreType.DMA,),
-    )(came.reshape(8 * NSRC, WIRE), own, oth)
+    )(x_rows, g_rows, own, oth)
     keep, send = call(
         weight_grads, (shape(8, 3 * BLK, HID), shape(8, 3 * BLK, HID)), 3
     )(x_rows, g_rows, grads)
@@ -339,12 +342,14 @@
     back = call(row_grads, shape(8 * NSRC, BACK), 4)(grads, dots, own, oth)
     one, two = shape(3 * BLK, HID), shape(6 * BLK, HID)
     s0, s2, s4, s6, right, left = call(add_cores, (one, one, one, one, two, two), 2)(keep, other)
-    right = shifted(right, 1)
     s4 = shifted(s4, 2)
     left = shifted(left, 7)
     back = exchange(back.reshape(NSRC, 8, BACK), ("z", "y"))
-    t2, t6 = call(join, (one, one), 5)(s2, right, s4, s6, left)
-    t2, t6 = shifted(t2, 2), shifted(t6, 6)
+    right = shifted(right, 1)
+    t6 = call(join_left, one, 2)(s6, left)
+    t6 = shifted(t6, 6)
+    t2 = call(join_right, one, 3)(s2, right, s4)
+    t2 = shifted(t2, 2)
     grad_gate, grad_up, grad_down = call(
         sum_chips, (shape(BLK, HID), shape(BLK, HID), shape(HID, BLK)), 5
     )(s0, right, left, t2, t6)

time: 138 us -> 133 us (0.964)
  local copies, waits for them, and re-layouts: 3.57 us -> 0.02 us
  starting transfers between devices: 85.7 us -> 83.8 us
    all_to_all x2, waiting for transfers between devices: 0.01 us -> 4.86 us  [exchange(): return lax.all_to_all(value, axis, split_axis=0, concat_axis=0, tiled=True)]
    unnamed x10, local copies, waits for them, and re-layouts: 3.57 us -> 0.02 us
    ppermute x1, waiting for transfers between devices: 3.42 us -> 0.01 us  [body(): oth = lax.ppermute(own, 'c', SWAP)]
    all_to_all x2, starting transfers between devices: 35.8 us -> 34.1 us  [exchange(): return lax.all_to_all(value, axis, split_axis=0, concat_axis=0, tiled=True)]
    pallas_call x3 -> x5, Pallas kernels: 3.98 us -> 3.26 us  [the longest x1 2.31 us: body(): call(forward, (shape(ROWS, 3 * HID), shape(ROWS, BLK), shape(8, SHARD, HI...]
where the time goes in v3:
time: 133 us
  starting transfers between devices  83.8 us (63%)
  waiting for transfers between devices  33.6 us (25%)
  Pallas kernels  14.2 us (11%)
    ppermute x12, starting transfers between devices, shifted(): return lax.ppermute(value, 'x', [(i, (i + by) % NX) for i in range(NX)])  45.9 us
    all_to_all x2, starting transfers between devices, exchange(): return lax.all_to_all(value, axis, split_axis=0, concat_axis=0, tiled=True)  34.1 us
    ppermute x12, waiting for transfers between devices, shifted(): return lax.ppermute(value, 'x', [(i, (i + by) % NX) for i in range(NX)])  28.7 us
    all_to_all x2, waiting for transfers between devices, exchange(): return lax.all_to_all(value, axis, split_axis=0, concat_axis=0, tiled=True)  4.86 us
    pallas_call x1, Pallas kernels, body(): call(send_rows, shape(NSRC, 8, WIRE), 4, limit=60)  2.76 us
  transfers between devices with their start and end apart: 16, of which 7 were waited for; matrix products, arithmetic and copies ran while one was open for 0% of the time, Pallas kernels for 5%

profile of v3, /device:TPU:4, one launch (start us, length us, event | category | flops | bytes accessed | tf_op | source)
XLA Modules:
  0.0 132.5 jit_solution(9401072843581279286)
XLA Ops:
  0.6 2.8 %shard_map.118 = bf16[64,8,1536]{2,1,0:T(8,128)(2,1)} custom-call(bf16[8,2048]{1,0:T(8,128)(2,1)} %tokens.1, bf16[8,2048]{1,0:T(8,128)(2,1)} %cotangent.1, s32[2,8]{1,0:T(2,128)} %bitcast.7, f32[8,8]{1,0:T(8,128)} %logits.3), custom_call_target="tpu_custom_call" | custom-call | tf_op jit(solution)/shard_map/pallas_call | solution.py:319
  3.4 23.5 %all-to-all-start = ((bf16[64,8,1536]{2,1,0:T(8,128)(2,1)}), bf16[64,8,1536]{2,1,0:T(8,128)(2,1)S(1)}, u32[]{:S(2)}, u32[]{:S(2)}) async-start(bf16[64,8,1536]{2,1,0:T(8,128)(2,1)} %shard_map.118), calls=%async_computation | async-start | bytes 3145728 | tf_op jit(solution)/shard_map/all_to_all | solution.py:311
  27.1 2.4 %collective-permute-start.4 = (bf16[392,256]{1,0:T(8,128)(2,1)S(1)}, bf16[392,256]{1,0:T(8,128)(2,1)S(1)}, u32[]{:S(2)}, u32[]{:S(2)}) collective-permute-start(bf16[392,256]{1,0:T(8,128)(2,1)S(1)} %shard_map.120.refs_0_), channel_id=1, source_target_pairs={{0,768},{128,896},{256,0},{384,128},{512,256},{640,384},{768,512},... | collective-permute-start | bytes 602120 | tf_op jit(solution)/shard_map/ppermute | solution.py:307
  29.5 5.5 %collective-permute-start.1 = (bf16[392,256]{1,0:T(8,128)(2,1)S(1)}, bf16[392,256]{1,0:T(8,128)(2,1)S(1)}, u32[]{:S(2)}, u32[]{:S(2)}) collective-permute-start(bf16[392,256]{1,0:T(8,128)(2,1)S(1)} %shard_map.120.refs_0_), channel_id=1, source_target_pairs={{0,256},{128,384},{256,512},{384,640},{512,768},{640,896},{768,0},... | collective-permute-start | bytes 602120 | tf_op jit(solution)/shard_map/ppermute | solution.py:307
  35.1 1.9 %collective-permute-start.6 = (bf16[392,256]{1,0:T(8,128)(2,1)S(1)}, bf16[392,256]{1,0:T(8,128)(2,1)S(1)}, u32[]{:S(2)}, u32[]{:S(2)}) collective-permute-start(bf16[392,256]{1,0:T(8,128)(2,1)S(1)} %shard_map.120.refs_0_), channel_id=1, source_target_pairs={{0,896},{128,0},{256,128},{384,256},{512,384},{640,512},{768,640},... | collective-permute-start | bytes 602120 | tf_op jit(solution)/shard_map/ppermute | solution.py:307
  37.0 3.9 %collective-permute-start = (bf16[392,256]{1,0:T(8,128)(2,1)S(1)}, bf16[392,256]{1,0:T(8,128)(2,1)S(1)}, u32[]{:S(2)}, u32[]{:S(2)}) collective-permute-start(bf16[392,256]{1,0:T(8,128)(2,1)S(1)} %shard_map.120.refs_0_), channel_id=1, source_target_pairs={{0,128},{128,256},{256,384},{384,512},{512,640},{640,768},{768,896... | collective-permute-start | bytes 602120 | tf_op jit(solution)/shard_map/ppermute | solution.py:307
  40.9 1.9 %collective-permute-done.4.refs_6_ = bf16[392,256]{1,0:T(8,128)(2,1)S(1)} collective-permute-done((bf16[392,256]{1,0:T(8,128)(2,1)S(1)}, bf16[392,256]{1,0:T(8,128)(2,1)S(1)}, u32[]{:S(2)}, u32[]{:S(2)}) %collective-permute-start.4) | collective-permute-done | bytes 200736 | tf_op jit(solution)/shard_map/ppermute | solution.py:307
  42.9 1.9 %collective-permute-start.5 = (bf16[392,256]{1,0:T(8,128)(2,1)S(1)}, bf16[392,256]{1,0:T(8,128)(2,1)S(1)}, u32[]{:S(2)}, u32[]{:S(2)}) collective-permute-start(bf16[392,256]{1,0:T(8,128)(2,1)S(1)} %collective-permute-done.4.refs_6_), channel_id=1, source_target_pairs={{0,896},{128,0},{256,128},{384,256},{512,384},{640,512},{768,640},... | collective-permute-start | bytes 602120 | tf_op jit(solution)/shard_map/ppermute | solution.py:307
  44.8 5.4 %collective-permute-start.3 = (bf16[392,256]{1,0:T(8,128)(2,1)S(1)}, bf16[392,256]{1,0:T(8,128)(2,1)S(1)}, u32[]{:S(2)}, u32[]{:S(2)}) collective-permute-start(bf16[392,256]{1,0:T(8,128)(2,1)S(1)} %collective-permute-done.1.refs_2_), channel_id=1, source_target_pairs={{0,256},{128,384},{256,512},{384,640},{512,768},{640,896},{768,0},... | collective-permute-start | bytes 602120 | tf_op jit(solution)/shard_map/ppermute | solution.py:307
  50.2 2.8 %collective-permute-start.2 = (bf16[392,256]{1,0:T(8,128)(2,1)S(1)}, bf16[392,256]{1,0:T(8,128)(2,1)S(1)}, u32[]{:S(2)}, u32[]{:S(2)}) collective-permute-start(bf16[392,256]{1,0:T(8,128)(2,1)S(1)} %collective-permute-done.1.refs_2_), channel_id=1, source_target_pairs={{0,128},{128,256},{256,384},{384,512},{512,640},{640,768},{768,896... | collective-permute-start | bytes 602120 | tf_op jit(solution)/shard_map/ppermute | solution.py:307
  53.0 5.7 %collective-permute-done.3.refs_4_ = bf16[392,256]{1,0:T(8,128)(2,1)S(1)} collective-permute-done((bf16[392,256]{1,0:T(8,128)(2,1)S(1)}, bf16[392,256]{1,0:T(8,128)(2,1)S(1)}, u32[]{:S(2)}, u32[]{:S(2)}) %collective-permute-start.3) | collective-permute-done | bytes 200736 | tf_op jit(solution)/shard_map/ppermute | solution.py:307
  58.8 2.6 %collective-permute-done.2.refs_3_ = bf16[392,256]{1,0:T(8,128)(2,1)S(1)} collective-permute-done((bf16[392,256]{1,0:T(8,128)(2,1)S(1)}, bf16[392,256]{1,0:T(8,128)(2,1)S(1)}, u32[]{:S(2)}, u32[]{:S(2)}) %collective-permute-start.2) | collective-permute-done | bytes 200736 | tf_op jit(solution)/shard_map/ppermute | solution.py:307
  61.4 0.1 shard_map.121.own
  61.5 1.9 %collective-permute-start.7 = (bf16[8,392,256]{2,1,0:T(8,128)(2,1)S(1)}, bf16[8,392,256]{2,1,0:T(8,128)(2,1)}, u32[]{:S(2)}, u32[]{:S(2)}) collective-permute-start(bf16[8,392,256]{2,1,0:T(8,128)(2,1)S(1)} %shard_map.121.own), channel_id=1, source_target_pairs={{0,64},{64,0},{1,65},{65,1},{2,66},{66,2},{3,67},{67,3},{4,68},{68... | collective-permute-start | bytes 4816904 | tf_op jit(solution)/shard_map/ppermute | solution.py:327
  63.4 4.9 %all-to-all-done = bf16[64,8,1536]{2,1,0:T(8,128)(2,1)S(1)} async-done(((bf16[64,8,1536]{2,1,0:T(8,128)(2,1)}), bf16[64,8,1536]{2,1,0:T(8,128)(2,1)S(1)}, u32[]{:S(2)}, u32[]{:S(2)}) %all-to-all-start) | async-done | bytes 1572896 | tf_op jit(solution)/shard_map/all_to_all | solution.py:311
  68.3 0.7 shard_map.119
  69.0 2.3 %shard_map.122 = (bf16[192,768]{1,0:T(8,128)(2,1)S(1)}, bf16[192,128]{1,0:T(8,128)(2,1)S(1)}, bf16[8,392,256]{2,1,0:T(8,128)(2,1)S(1)}) custom-call(bf16[192,2048]{1,0:T(8,128)(2,1)S(1)} %get-tuple-element.25.x_rows, bf16[192,2048]{1,0:T(8,128)(2,1)S(1)} %get-tuple-element.26.g_rows, bf16[8,392,256]{2,1,0:T(8,128)(2,1)S(1)} %shard_map.121.own, ...), custom_call_target="tpu_custom_call" | custom-call | tf_op jit(solution)/shard_map/pallas_call | solution.py:331
  71.3 2.0 %shard_map.125 = (bf16[8,384,256]{2,1,0:T(8,128)(2,1)S(1)}, bf16[8,384,256]{2,1,0:T(8,128)(2,1)}) custom-call(bf16[192,2048]{1,0:T(8,128)(2,1)S(1)} %get-tuple-element.25.x_rows, bf16[192,2048]{1,0:T(8,128)(2,1)S(1)} %get-tuple-element.26.g_rows, bf16[192,768]{1,0:T(8,128)(2,1)S(1)} %get-tuple-element.27.grads), custom_call_target="tpu_custom_call" | custom-call | tf_op jit(solution)/shard_map/pallas_call | solution.py:338
  73.3 1.9 %collective-permute-start.8 = (bf16[8,384,256]{2,1,0:T(8,128)(2,1)}, bf16[8,384,256]{2,1,0:T(8,128)(2,1)}, u32[]{:S(2)}, u32[]{:S(2)}) collective-permute-start(bf16[8,384,256]{2,1,0:T(8,128)(2,1)} %get-tuple-element.34), channel_id=1, source_target_pairs={{0,64},{64,0},{1,65},{65,1},{2,66},{66,2},{3,67},{67,3},{4,68},{68... | collective-permute-start | bytes 4718600 | tf_op jit(solution)/shard_map/ppermute | solution.py:341
  75.2 2.6 %shard_map.123 = bf16[512,896]{1,0:T(8,128)(2,1)} custom-call(bf16[192,768]{1,0:T(8,128)(2,1)S(1)} %get-tuple-element.27.grads, bf16[192,128]{1,0:T(8,128)(2,1)S(1)} %get-tuple-element.28.dots, bf16[8,392,256]{2,1,0:T(8,128)(2,1)S(1)} %shard_map.121.own, bf16[8,392,256]{2,1,0:T(8,128)(2,1)S(1)} %get-tuple-element.29.oth), custom_call_target="tpu_custom_call" | custom-call | tf_op jit(solution)/shard_map/pallas_call | solution.py:342
  77.8 10.5 %all-to-all-start.1 = ((bf16[64,8,896]{2,1,0:T(8,128)(2,1)}), bf16[64,8,896]{2,1,0:T(8,128)(2,1)S(1)}, u32[]{:S(2)}, u32[]{:S(2)}) async-start(bf16[64,8,896]{2,1,0:T(8,128)(2,1)} %bitcast.2), calls=%async_computation.1 | async-start | bytes 1835008 | tf_op jit(solution)/shard_map/all_to_all | solution.py:311
  88.4 1.8 %shard_map.126 = (bf16[384,256]{1,0:T(8,128)(2,1)S(1)}, bf16[384,256]{1,0:T(8,128)(2,1)S(1)}, bf16[384,256]{1,0:T(8,128)(2,1)S(1)}, bf16[384,256]{1,0:T(8,128)(2...) custom-call(bf16[8,384,256]{2,1,0:T(8,128)(2,1)S(1)} %get-tuple-element.33.keep, ...), custom_call_target="tpu_custom_call" | custom-call | tf_op jit(solution)/shard_map/pallas_call | solution.py:344
  90.2 3.9 %collective-permute-start.9 = (bf16[768,256]{1,0:T(8,128)(2,1)S(1)}, bf16[768,256]{1,0:T(8,128)(2,1)S(1)}, u32[]{:S(2)}, u32[]{:S(2)}) collective-permute-start(bf16[768,256]{1,0:T(8,128)(2,1)S(1)} %get-tuple-element.36), channel_id=1, source_target_pairs={{0,128},{128,256},{256,384},{384,512},{512,640},{640,768},{768,896... | collective-permute-start | bytes 1179656 | tf_op jit(solution)/shard_map/ppermute | solution.py:307
  94.0 2.0 %collective-permute-start.10 = (bf16[768,256]{1,0:T(8,128)(2,1)S(1)}, bf16[768,256]{1,0:T(8,128)(2,1)S(1)}, u32[]{:S(2)}, u32[]{:S(2)}) collective-permute-start(bf16[768,256]{1,0:T(8,128)(2,1)S(1)} %get-tuple-element.37), channel_id=1, source_target_pairs={{0,896},{128,0},{256,128},{384,256},{512,384},{640,512},{768,640},... | collective-permute-start | bytes 1179656 | tf_op jit(solution)/shard_map/ppermute | solution.py:307
  96.0 7.7 %collective-permute-start.11 = (bf16[384,256]{1,0:T(8,128)(2,1)S(1)}, bf16[384,256]{1,0:T(8,128)(2,1)S(1)}, u32[]{:S(2)}, u32[]{:S(2)}) collective-permute-start(bf16[384,256]{1,0:T(8,128)(2,1)S(1)} %get-tuple-element.39), channel_id=1, source_target_pairs={{0,256},{128,384},{256,512},{384,640},{512,768},{640,896},{768,0},... | collective-permute-start | bytes 589832 | tf_op jit(solution)/shard_map/ppermute | solution.py:307
  103.7 7.4 %collective-permute-done.11.s4 = bf16[384,256]{1,0:T(8,128)(2,1)S(1)} collective-permute-done((bf16[384,256]{1,0:T(8,128)(2,1)S(1)}, bf16[384,256]{1,0:T(8,128)(2,1)S(1)}, u32[]{:S(2)}, u32[]{:S(2)}) %collective-permute-start.11) | collective-permute-done | bytes 196640 | tf_op jit(solution)/shard_map/ppermute | solution.py:307
  111.2 6.6 %collective-permute-start.12 = (bf16[384,256]{1,0:T(8,128)(2,1)S(1)}, bf16[384,256]{1,0:T(8,128)(2,1)S(1)}, u32[]{:S(2)}, u32[]{:S(2)}) collective-permute-start(bf16[384,256]{1,0:T(8,128)(2,1)S(1)} %shard_map.127), channel_id=1, source_target_pairs={{0,256},{128,384},{256,512},{384,640},{512,768},{640,896},{768,0},... | collective-permute-start | bytes 589832 | tf_op jit(solution)/shard_map/ppermute | solution.py:307
  117.8 1.9 %collective-permute-start.13 = (bf16[384,256]{1,0:T(8,128)(2,1)S(1)}, bf16[384,256]{1,0:T(8,128)(2,1)S(1)}, u32[]{:S(2)}, u32[]{:S(2)}) collective-permute-start(bf16[384,256]{1,0:T(8,128)(2,1)S(1)} %shard_map.128), channel_id=1, source_target_pairs={{0,768},{128,896},{256,0},{384,128},{512,256},{640,384},{768,512},... | collective-permute-start | bytes 589832 | tf_op jit(solution)/shard_map/ppermute | solution.py:307
  119.8 0.9 shard_map.124
  120.7 4.2 %collective-permute-done.12.t2 = bf16[384,256]{1,0:T(8,128)(2,1)S(1)} collective-permute-done((bf16[384,256]{1,0:T(8,128)(2,1)S(1)}, bf16[384,256]{1,0:T(8,128)(2,1)S(1)}, u32[]{:S(2)}, u32[]{:S(2)}) %collective-permute-start.12) | collective-permute-done | bytes 196640 | tf_op jit(solution)/shard_map/ppermute | solution.py:307
  125.0 6.8 %collective-permute-done.13.t6 = bf16[384,256]{1,0:T(8,128)(2,1)S(1)} collective-permute-done((bf16[384,256]{1,0:T(8,128)(2,1)S(1)}, bf16[384,256]{1,0:T(8,128)(2,1)S(1)}, u32[]{:S(2)}, u32[]{:S(2)}) %collective-permute-start.13) | collective-permute-done | bytes 196640 | tf_op jit(solution)/shard_map/ppermute | solution.py:307
  131.7 0.8 shard_map.129
  (22 shorter events, 0.3 us)
Async XLA Ops:
  3.4 23.6 %copy-start = (bf16[128,256]{1,0:T(8,128)(2,1)S(1)}, bf16[128,256]{1,0:T(8,128)(2,1)}, u32[]{:S(2)}) copy-start(bf16[128,256]{1,0:T(8,128)(2,1)} %w_gate.1) | copy-start | bytes 196612
  3.4 23.6 %copy-start.1 = (bf16[128,256]{1,0:T(8,128)(2,1)S(1)}, bf16[128,256]{1,0:T(8,128)(2,1)}, u32[]{:S(2)}) copy-start(bf16[128,256]{1,0:T(8,128)(2,1)} %w_up.1) | copy-start | bytes 196612
  3.4 23.6 %copy-start.2 = (bf16[256,128]{1,0:T(8,128)(2,1)S(1)}, bf16[256,128]{1,0:T(8,128)(2,1)}, u32[]{:S(2)}) copy-start(bf16[256,128]{1,0:T(8,128)(2,1)} %w_down.1) | copy-start | bytes 196612
  3.4 23.6 %copy-start.4 = (s32[8,2]{0,1:T(2,128)S(1)}, s32[8,2]{0,1:T(2,128)}, u32[]{:S(2)}) copy-start(s32[8,2]{0,1:T(2,128)} %param.9) | copy-start | bytes 196
  3.4 64.9 %all-to-all-start = ((bf16[64,8,1536]{2,1,0:T(8,128)(2,1)}), bf16[64,8,1536]{2,1,0:T(8,128)(2,1)S(1)}, u32[]{:S(2)}, u32[]{:S(2)}) async-start(bf16[64,8,1536]{2,1,0:T(8,128)(2,1)} %shard_map.118), calls=%async_computation | async-start | bytes 3145728 | tf_op jit(solution)/shard_map/all_to_all | solution.py:311
  27.1 15.8 %collective-permute-start.4 = (bf16[392,256]{1,0:T(8,128)(2,1)S(1)}, bf16[392,256]{1,0:T(8,128)(2,1)S(1)}, u32[]{:S(2)}, u32[]{:S(2)}) collective-permute-start(bf16[392,256]{1,0:T(8,128)(2,1)S(1)} %shard_map.120.refs_0_), channel_id=1, source_target_pairs={{0,768},{128,896},{256,0},{384,128},{512,256},{640,384},{768,512},... | collective-permute-start | bytes 602120 | tf_op jit(solution)/shard_map/ppermute | solution.py:307
  29.5 15.3 %collective-permute-start.1 = (bf16[392,256]{1,0:T(8,128)(2,1)S(1)}, bf16[392,256]{1,0:T(8,128)(2,1)S(1)}, u32[]{:S(2)}, u32[]{:S(2)}) collective-permute-start(bf16[392,256]{1,0:T(8,128)(2,1)S(1)} %shard_map.120.refs_0_), channel_id=1, source_target_pairs={{0,256},{128,384},{256,512},{384,640},{512,768},{640,896},{768,0},... | collective-permute-start | bytes 602120 | tf_op jit(solution)/shard_map/ppermute | solution.py:307
  35.1 17.9 %collective-permute-start.6 = (bf16[392,256]{1,0:T(8,128)(2,1)S(1)}, bf16[392,256]{1,0:T(8,128)(2,1)S(1)}, u32[]{:S(2)}, u32[]{:S(2)}) collective-permute-start(bf16[392,256]{1,0:T(8,128)(2,1)S(1)} %shard_map.120.refs_0_), channel_id=1, source_target_pairs={{0,896},{128,0},{256,128},{384,256},{512,384},{640,512},{768,640},... | collective-permute-start | bytes 602120 | tf_op jit(solution)/shard_map/ppermute | solution.py:307
  37.0 16.0 %collective-permute-start = (bf16[392,256]{1,0:T(8,128)(2,1)S(1)}, bf16[392,256]{1,0:T(8,128)(2,1)S(1)}, u32[]{:S(2)}, u32[]{:S(2)}) collective-permute-start(bf16[392,256]{1,0:T(8,128)(2,1)S(1)} %shard_map.120.refs_0_), channel_id=1, source_target_pairs={{0,128},{128,256},{256,384},{384,512},{512,640},{640,768},{768,896... | collective-permute-start | bytes 602120 | tf_op jit(solution)/shard_map/ppermute | solution.py:307
  42.9 10.2 %collective-permute-start.5 = (bf16[392,256]{1,0:T(8,128)(2,1)S(1)}, bf16[392,256]{1,0:T(8,128)(2,1)S(1)}, u32[]{:S(2)}, u32[]{:S(2)}) collective-permute-start(bf16[392,256]{1,0:T(8,128)(2,1)S(1)} %collective-permute-done.4.refs_6_), channel_id=1, source_target_pairs={{0,896},{128,0},{256,128},{384,256},{512,384},{640,512},{768,640},... | collective-permute-start | bytes 602120 | tf_op jit(solution)/shard_map/ppermute | solution.py:307
  44.8 14.0 %collective-permute-start.3 = (bf16[392,256]{1,0:T(8,128)(2,1)S(1)}, bf16[392,256]{1,0:T(8,128)(2,1)S(1)}, u32[]{:S(2)}, u32[]{:S(2)}) collective-permute-start(bf16[392,256]{1,0:T(8,128)(2,1)S(1)} %collective-permute-done.1.refs_2_), channel_id=1, source_target_pairs={{0,256},{128,384},{256,512},{384,640},{512,768},{640,896},{768,0},... | collective-permute-start | bytes 602120 | tf_op jit(solution)/shard_map/ppermute | solution.py:307
  50.2 11.2 %collective-permute-start.2 = (bf16[392,256]{1,0:T(8,128)(2,1)S(1)}, bf16[392,256]{1,0:T(8,128)(2,1)S(1)}, u32[]{:S(2)}, u32[]{:S(2)}) collective-permute-start(bf16[392,256]{1,0:T(8,128)(2,1)S(1)} %collective-permute-done.1.refs_2_), channel_id=1, source_target_pairs={{0,128},{128,256},{256,384},{384,512},{512,640},{640,768},{768,896... | collective-permute-start | bytes 602120 | tf_op jit(solution)/shard_map/ppermute | solution.py:307
  61.5 7.5 %collective-permute-start.7 = (bf16[8,392,256]{2,1,0:T(8,128)(2,1)S(1)}, bf16[8,392,256]{2,1,0:T(8,128)(2,1)}, u32[]{:S(2)}, u32[]{:S(2)}) collective-permute-start(bf16[8,392,256]{2,1,0:T(8,128)(2,1)S(1)} %shard_map.121.own), channel_id=1, source_target_pairs={{0,64},{64,0},{1,65},{65,1},{2,66},{66,2},{3,67},{67,3},{4,68},{68... | collective-permute-start | bytes 4816904 | tf_op jit(solution)/shard_map/ppermute | solution.py:327
  73.3 15.1 %collective-permute-start.8 = (bf16[8,384,256]{2,1,0:T(8,128)(2,1)}, bf16[8,384,256]{2,1,0:T(8,128)(2,1)}, u32[]{:S(2)}, u32[]{:S(2)}) collective-permute-start(bf16[8,384,256]{2,1,0:T(8,128)(2,1)} %get-tuple-element.34), channel_id=1, source_target_pairs={{0,64},{64,0},{1,65},{65,1},{2,66},{66,2},{3,67},{67,3},{4,68},{68... | collective-permute-start | bytes 4718600 | tf_op jit(solution)/shard_map/ppermute | solution.py:341
  77.8 41.9 %all-to-all-start.1 = ((bf16[64,8,896]{2,1,0:T(8,128)(2,1)}), bf16[64,8,896]{2,1,0:T(8,128)(2,1)S(1)}, u32[]{:S(2)}, u32[]{:S(2)}) async-start(bf16[64,8,896]{2,1,0:T(8,128)(2,1)} %bitcast.2), calls=%async_computation.1 | async-start | bytes 1835008 | tf_op jit(solution)/shard_map/all_to_all | solution.py:311
  90.1 29.6 %copy-start.3 = (f32[8,8]{1,0:T(8,128)S(1)}, f32[8,8]{1,0:T(8,128)}, u32[]{:S(2)}) copy-start(f32[8,8]{1,0:T(8,128)} %logits.3) | copy-start | bytes 772
  90.2 21.0 %collective-permute-start.9 = (bf16[768,256]{1,0:T(8,128)(2,1)S(1)}, bf16[768,256]{1,0:T(8,128)(2,1)S(1)}, u32[]{:S(2)}, u32[]{:S(2)}) collective-permute-start(bf16[768,256]{1,0:T(8,128)(2,1)S(1)} %get-tuple-element.36), channel_id=1, source_target_pairs={{0,128},{128,256},{256,384},{384,512},{512,640},{640,768},{768,896... | collective-permute-start | bytes 1179656 | tf_op jit(solution)/shard_map/ppermute | solution.py:307
  94.0 23.8 %collective-permute-start.10 = (bf16[768,256]{1,0:T(8,128)(2,1)S(1)}, bf16[768,256]{1,0:T(8,128)(2,1)S(1)}, u32[]{:S(2)}, u32[]{:S(2)}) collective-permute-start(bf16[768,256]{1,0:T(8,128)(2,1)S(1)} %get-tuple-element.37), channel_id=1, source_target_pairs={{0,896},{128,0},{256,128},{384,256},{512,384},{640,512},{768,640},... | collective-permute-start | bytes 1179656 | tf_op jit(solution)/shard_map/ppermute | solution.py:307
  96.0 15.1 %collective-permute-start.11 = (bf16[384,256]{1,0:T(8,128)(2,1)S(1)}, bf16[384,256]{1,0:T(8,128)(2,1)S(1)}, u32[]{:S(2)}, u32[]{:S(2)}) collective-permute-start(bf16[384,256]{1,0:T(8,128)(2,1)S(1)} %get-tuple-element.39), channel_id=1, source_target_pairs={{0,256},{128,384},{256,512},{384,640},{512,768},{640,896},{768,0},... | collective-permute-start | bytes 589832 | tf_op jit(solution)/shard_map/ppermute | solution.py:307
  111.2 13.8 %collective-permute-start.12 = (bf16[384,256]{1,0:T(8,128)(2,1)S(1)}, bf16[384,256]{1,0:T(8,128)(2,1)S(1)}, u32[]{:S(2)}, u32[]{:S(2)}) collective-permute-start(bf16[384,256]{1,0:T(8,128)(2,1)S(1)} %shard_map.127), channel_id=1, source_target_pairs={{0,256},{128,384},{256,512},{384,640},{512,768},{640,896},{768,0},... | collective-permute-start | bytes 589832 | tf_op jit(solution)/shard_map/ppermute | solution.py:307
  117.8 13.9 %collective-permute-start.13 = (bf16[384,256]{1,0:T(8,128)(2,1)S(1)}, bf16[384,256]{1,0:T(8,128)(2,1)S(1)}, u32[]{:S(2)}, u32[]{:S(2)}) collective-permute-start(bf16[384,256]{1,0:T(8,128)(2,1)S(1)} %shard_map.128), channel_id=1, source_target_pairs={{0,768},{128,896},{256,0},{384,128},{512,256},{640,384},{768,512},... | collective-permute-start | bytes 589832 | tf_op jit(solution)/shard_map/ppermute | solution.py:307

commit v4 on v3

--- a/solution.py
+++ b/solution.py
@@ -230,38 +230,27 @@
             ref[:, k * BLK : (k + 1) * BLK, :] = v.astype(bf16).reshape(8, BLK, HID)
 
 
-def add_cores(keep, came, s0, s2, s4, s6, right, left):
+def add_cores(keep, came, *outs):
     chip = lax.axis_index("x")
-
-    def total(k):
+    for k in range(8):
         at = lax.rem(chip + k, 8)
-        return (keep[at].astype(f32) + came[at].astype(f32)).astype(bf16)
-
-    right[0 : 3 * BLK] = total(3)
-    right[3 * BLK :] = total(1)
-    s4[...] = total(4)
-    left[0 : 3 * BLK] = total(5)
-    left[3 * BLK :] = total(7)
-    s2[...] = total(2)
-    s6[...] = total(6)
-    s0[...] = total(0)
+        outs[k][...] = (keep[at].astype(f32) + came[at].astype(f32)).astype(bf16)
 
 
 def join_right(s2, right, s4, t2):
-    near = right[0 : 3 * BLK].astype(f32)
-    t2[...] = (s2[...].astype(f32) + near + s4[...].astype(f32)).astype(bf16)
+    total = s2[...].astype(f32) + right[...].astype(f32) + s4[...].astype(f32)
+    t2[...] = total.astype(bf16)
 
 
 def join_left(s6, left, t6):
-    t6[...] = (s6[...].astype(f32) + left[0 : 3 * BLK].astype(f32)).astype(bf16)
-
-
-def sum_chips(s0, right, left, t2, t6, gate, up, down):
+    t6[...] = (s6[...].astype(f32) + left[...].astype(f32)).astype(bf16)
+
+
+def sum_chips(s0, e1, e7, t2, t6, gate, up, down):
     for k, ref in ((0, gate), (1, up), (2, down)):
         lo, hi = k * BLK, (k + 1) * BLK
         total = s0[lo:hi].astype(f32) + t2[lo:hi].astype(f32) + t6[lo:hi].astype(f32)
-        lo, hi = lo + 3 * BLK, hi + 3 * BLK
-        total = total + right[lo:hi].astype(f32) + left[lo:hi].astype(f32)
+        total = total + e1[lo:hi].astype(f32) + e7[lo:hi].astype(f32)
         ref[...] = (jnp.transpose(total) if k == 2 else total).astype(bf16)
 
 
@@ -340,19 +329,21 @@
     )(x_rows, g_rows, grads)
     other = lax.ppermute(send, "c", SWAP)
     back = call(row_grads, shape(8 * NSRC, BACK), 4)(grads, dots, own, oth)
-    one, two = shape(3 * BLK, HID), shape(6 * BLK, HID)
-    s0, s2, s4, s6, right, left = call(add_cores, (one, one, one, one, two, two), 2)(keep, other)
-    s4 = shifted(s4, 2)
-    left = shifted(left, 7)
+    one = shape(3 * BLK, HID)
+    s = call(add_cores, (one,) * 8, 2)(keep, other)
+    far = shifted(s[4], 2)
+    right = shifted(s[3], 1)
     back = exchange(back.reshape(NSRC, 8, BACK), ("z", "y"))
-    right = shifted(right, 1)
-    t6 = call(join_left, one, 2)(s6, left)
+    left = shifted(s[5], 7)
+    t2 = call(join_right, one, 3)(s[2], right, far)
+    t2 = shifted(t2, 2)
+    t6 = call(join_left, one, 2)(s[6], left)
     t6 = shifted(t6, 6)
-    t2 = call(join_right, one, 3)(s2, right, s4)
-    t2 = shifted(t2, 2)
+    e1 = shifted(s[1], 1)
+    e7 = shifted(s[7], 7)
     grad_gate, grad_up, grad_down = call(
         sum_chips, (shape(BLK, HID), shape(BLK, HID), shape(HID, BLK)), 5
-    )(s0, right, left, t2, t6)
+    )(s[0], e1, e7, t2, t6)
     grad_tokens, route_dot, aux_grad = call(
         finish, (shape(8, DM), shape(2, 8, dtype=f32), shape(8, 8, dtype=f32)), 3
     )(back.reshape(8 * NSRC, BACK), routes_t, logits)

time: 133 us -> 130 us (0.977)
  the two profiles are of different devices: /device:TPU:4 before, /device:TPU:2 now
where the time goes in v4:
time: 130 us; the launch traced here: 129 us
  starting transfers between devices  86.3 us (66%)
  waiting for transfers between devices  26.7 us (21%)
  Pallas kernels  14.8 us (11%)
    ppermute x14, starting transfers between devices, shifted(): return lax.ppermute(value, 'x', [(i, (i + by) % NX) for i in range(NX)])  48 us
    all_to_all x2, starting transfers between devices, exchange(): return lax.all_to_all(value, axis, split_axis=0, concat_axis=0, tiled=True)  34.5 us
    ppermute x14, waiting for transfers between devices, shifted(): return lax.ppermute(value, 'x', [(i, (i + by) % NX) for i in range(NX)])  22.3 us
    all_to_all x2, waiting for transfers between devices, exchange(): return lax.all_to_all(value, axis, split_axis=0, concat_axis=0, tiled=True)  4.41 us
    pallas_call x1, Pallas kernels, body(): call(send_rows, shape(NSRC, 8, WIRE), 4, limit=60)  2.76 us
    pallas_call x1, Pallas kernels, body(): back = call(row_grads, shape(8 * NSRC, BACK), 4)(grads, dots, own, oth)  2.64 us
  transfers between devices with their start and end apart: 18, of which 7 were waited for; matrix products, arithmetic and copies ran while one was open for 0% of the time, Pallas kernels for 5%

profile of v4, /device:TPU:2, one launch (start us, length us, event | category | flops | bytes accessed | tf_op | source)
XLA Modules:
  0.0 128.8 jit_solution(14952632153830681178)
XLA Ops:
  0.6 2.8 %shard_map.118 = bf16[64,8,1536]{2,1,0:T(8,128)(2,1)} custom-call(bf16[8,2048]{1,0:T(8,128)(2,1)} %tokens.1, bf16[8,2048]{1,0:T(8,128)(2,1)} %cotangent.1, s32[2,8]{1,0:T(2,128)} %bitcast.7, f32[8,8]{1,0:T(8,128)} %logits.3), custom_call_target="tpu_custom_call" | custom-call | tf_op jit(solution)/shard_map/pallas_call | solution.py:308
  3.4 23.6 %all-to-all-start = ((bf16[64,8,1536]{2,1,0:T(8,128)(2,1)}), bf16[64,8,1536]{2,1,0:T(8,128)(2,1)S(1)}, u32[]{:S(2)}, u32[]{:S(2)}) async-start(bf16[64,8,1536]{2,1,0:T(8,128)(2,1)} %shard_map.118), calls=%async_computation | async-start | bytes 3145728 | tf_op jit(solution)/shard_map/all_to_all | solution.py:300
  27.1 4.8 %collective-permute-start.4 = (bf16[392,256]{1,0:T(8,128)(2,1)S(1)}, bf16[392,256]{1,0:T(8,128)(2,1)S(1)}, u32[]{:S(2)}, u32[]{:S(2)}) collective-permute-start(bf16[392,256]{1,0:T(8,128)(2,1)S(1)} %shard_map.120.refs_0_), channel_id=1, source_target_pairs={{0,768},{128,896},{256,0},{384,128},{512,256},{640,384},{768,512},... | collective-permute-start | bytes 602120 | tf_op jit(solution)/shard_map/ppermute | solution.py:296
  31.9 2.0 %collective-permute-start.1 = (bf16[392,256]{1,0:T(8,128)(2,1)S(1)}, bf16[392,256]{1,0:T(8,128)(2,1)S(1)}, u32[]{:S(2)}, u32[]{:S(2)}) collective-permute-start(bf16[392,256]{1,0:T(8,128)(2,1)S(1)} %shard_map.120.refs_0_), channel_id=1, source_target_pairs={{0,256},{128,384},{256,512},{384,640},{512,768},{640,896},{768,0},... | collective-permute-start | bytes 602120 | tf_op jit(solution)/shard_map/ppermute | solution.py:296
  33.9 3.3 %collective-permute-start.6 = (bf16[392,256]{1,0:T(8,128)(2,1)S(1)}, bf16[392,256]{1,0:T(8,128)(2,1)S(1)}, u32[]{:S(2)}, u32[]{:S(2)}) collective-permute-start(bf16[392,256]{1,0:T(8,128)(2,1)S(1)} %shard_map.120.refs_0_), channel_id=1, source_target_pairs={{0,896},{128,0},{256,128},{384,256},{512,384},{640,512},{768,640},... | collective-permute-start | bytes 602120 | tf_op jit(solution)/shard_map/ppermute | solution.py:296
  37.2 3.2 %collective-permute-start = (bf16[392,256]{1,0:T(8,128)(2,1)S(1)}, bf16[392,256]{1,0:T(8,128)(2,1)S(1)}, u32[]{:S(2)}, u32[]{:S(2)}) collective-permute-start(bf16[392,256]{1,0:T(8,128)(2,1)S(1)} %shard_map.120.refs_0_), channel_id=1, source_target_pairs={{0,128},{128,256},{256,384},{384,512},{512,640},{640,768},{768,896... | collective-permute-start | bytes 602120 | tf_op jit(solution)/shard_map/ppermute | solution.py:296
  40.4 3.8 %collective-permute-start.5 = (bf16[392,256]{1,0:T(8,128)(2,1)S(1)}, bf16[392,256]{1,0:T(8,128)(2,1)S(1)}, u32[]{:S(2)}, u32[]{:S(2)}) collective-permute-start(bf16[392,256]{1,0:T(8,128)(2,1)S(1)} %collective-permute-done.4.refs_6_), channel_id=1, source_target_pairs={{0,896},{128,0},{256,128},{384,256},{512,384},{640,512},{768,640},... | collective-permute-start | bytes 602120 | tf_op jit(solution)/shard_map/ppermute | solution.py:296
  44.3 3.5 %collective-permute-done.1.refs_2_ = bf16[392,256]{1,0:T(8,128)(2,1)S(1)} collective-permute-done((bf16[392,256]{1,0:T(8,128)(2,1)S(1)}, bf16[392,256]{1,0:T(8,128)(2,1)S(1)}, u32[]{:S(2)}, u32[]{:S(2)}) %collective-permute-start.1) | collective-permute-done | bytes 200736 | tf_op jit(solution)/shard_map/ppermute | solution.py:296
  47.8 1.9 %collective-permute-start.3 = (bf16[392,256]{1,0:T(8,128)(2,1)S(1)}, bf16[392,256]{1,0:T(8,128)(2,1)S(1)}, u32[]{:S(2)}, u32[]{:S(2)}) collective-permute-start(bf16[392,256]{1,0:T(8,128)(2,1)S(1)} %collective-permute-done.1.refs_2_), channel_id=1, source_target_pairs={{0,256},{128,384},{256,512},{384,640},{512,768},{640,896},{768,0},... | collective-permute-start | bytes 602120 | tf_op jit(solution)/shard_map/ppermute | solution.py:296
  49.7 3.9 %collective-permute-start.2 = (bf16[392,256]{1,0:T(8,128)(2,1)S(1)}, bf16[392,256]{1,0:T(8,128)(2,1)S(1)}, u32[]{:S(2)}, u32[]{:S(2)}) collective-permute-start(bf16[392,256]{1,0:T(8,128)(2,1)S(1)} %collective-permute-done.1.refs_2_), channel_id=1, source_target_pairs={{0,128},{128,256},{256,384},{384,512},{512,640},{640,768},{768,896... | collective-permute-start | bytes 602120 | tf_op jit(solution)/shard_map/ppermute | solution.py:296
  53.6 6.5 %collective-permute-done.3.refs_4_ = bf16[392,256]{1,0:T(8,128)(2,1)S(1)} collective-permute-done((bf16[392,256]{1,0:T(8,128)(2,1)S(1)}, bf16[392,256]{1,0:T(8,128)(2,1)S(1)}, u32[]{:S(2)}, u32[]{:S(2)}) %collective-permute-start.3) | collective-permute-done | bytes 200736 | tf_op jit(solution)/shard_map/ppermute | solution.py:296
  60.2 1.7 %collective-permute-done.2.refs_3_ = bf16[392,256]{1,0:T(8,128)(2,1)S(1)} collective-permute-done((bf16[392,256]{1,0:T(8,128)(2,1)S(1)}, bf16[392,256]{1,0:T(8,128)(2,1)S(1)}, u32[]{:S(2)}, u32[]{:S(2)}) %collective-permute-start.2) | collective-permute-done | bytes 200736 | tf_op jit(solution)/shard_map/ppermute | solution.py:296
  61.9 1.9 %collective-permute-start.7 = (bf16[8,392,256]{2,1,0:T(8,128)(2,1)S(1)}, bf16[8,392,256]{2,1,0:T(8,128)(2,1)}, u32[]{:S(2)}, u32[]{:S(2)}) collective-permute-start(bf16[8,392,256]{2,1,0:T(8,128)(2,1)S(1)} %shard_map.121.own), channel_id=1, source_target_pairs={{0,64},{64,0},{1,65},{65,1},{2,66},{66,2},{3,67},{67,3},{4,68},{68... | collective-permute-start | bytes 4816904 | tf_op jit(solution)/shard_map/ppermute | solution.py:316
  63.9 4.4 %all-to-all-done = bf16[64,8,1536]{2,1,0:T(8,128)(2,1)S(1)} async-done(((bf16[64,8,1536]{2,1,0:T(8,128)(2,1)}), bf16[64,8,1536]{2,1,0:T(8,128)(2,1)S(1)}, u32[]{:S(2)}, u32[]{:S(2)}) %all-to-all-start) | async-done | bytes 1572896 | tf_op jit(solution)/shard_map/all_to_all | solution.py:300
  69.0 2.3 %shard_map.122 = (bf16[192,768]{1,0:T(8,128)(2,1)S(1)}, bf16[192,128]{1,0:T(8,128)(2,1)S(1)}, bf16[8,392,256]{2,1,0:T(8,128)(2,1)S(1)}) custom-call(bf16[192,2048]{1,0:T(8,128)(2,1)S(1)} %get-tuple-element.27.x_rows, bf16[192,2048]{1,0:T(8,128)(2,1)S(1)} %get-tuple-element.28.g_rows, bf16[8,392,256]{2,1,0:T(8,128)(2,1)S(1)} %shard_map.121.own, ...), custom_call_target="tpu_custom_call" | custom-call | tf_op jit(solution)/shard_map/pallas_call | solution.py:320
  71.3 1.9 %shard_map.125 = (bf16[8,384,256]{2,1,0:T(8,128)(2,1)S(1)}, bf16[8,384,256]{2,1,0:T(8,128)(2,1)}) custom-call(bf16[192,2048]{1,0:T(8,128)(2,1)S(1)} %get-tuple-element.27.x_rows, bf16[192,2048]{1,0:T(8,128)(2,1)S(1)} %get-tuple-element.28.g_rows, bf16[192,768]{1,0:T(8,128)(2,1)S(1)} %get-tuple-element.29.grads), custom_call_target="tpu_custom_call" | custom-call | tf_op jit(solution)/shard_map/pallas_call | solution.py:327
  73.3 1.9 %collective-permute-start.8 = (bf16[8,384,256]{2,1,0:T(8,128)(2,1)}, bf16[8,384,256]{2,1,0:T(8,128)(2,1)}, u32[]{:S(2)}, u32[]{:S(2)}) collective-permute-start(bf16[8,384,256]{2,1,0:T(8,128)(2,1)} %get-tuple-element.36), channel_id=1, source_target_pairs={{0,64},{64,0},{1,65},{65,1},{2,66},{66,2},{3,67},{67,3},{4,68},{68... | collective-permute-start | bytes 4718600 | tf_op jit(solution)/shard_map/ppermute | solution.py:330
  75.2 2.6 %shard_map.123 = bf16[512,896]{1,0:T(8,128)(2,1)} custom-call(bf16[192,768]{1,0:T(8,128)(2,1)S(1)} %get-tuple-element.29.grads, bf16[192,128]{1,0:T(8,128)(2,1)S(1)} %get-tuple-element.30.dots, bf16[8,392,256]{2,1,0:T(8,128)(2,1)S(1)} %shard_map.121.own, bf16[8,392,256]{2,1,0:T(8,128)(2,1)S(1)} %get-tuple-element.31.oth), custom_call_target="tpu_custom_call" | custom-call | tf_op jit(solution)/shard_map/pallas_call | solution.py:331
  77.8 11.0 %all-to-all-start.1 = ((bf16[64,8,896]{2,1,0:T(8,128)(2,1)}), bf16[64,8,896]{2,1,0:T(8,128)(2,1)S(1)}, u32[]{:S(2)}, u32[]{:S(2)}) async-start(bf16[64,8,896]{2,1,0:T(8,128)(2,1)} %bitcast.2), calls=%async_computation.1 | async-start | bytes 1835008 | tf_op jit(solution)/shard_map/all_to_all | solution.py:300
  88.8 2.4 %shard_map.126 = (bf16[384,256]{1,0:T(8,128)(2,1)S(1)}, bf16[384,256]{1,0:T(8,128)(2,1)}, bf16[384,256]{1,0:T(8,128)(2,1)S(1)}, bf16[384,256]{1,0:T(8,128)(2,1)S...) custom-call(bf16[8,384,256]{2,1,0:T(8,128)(2,1)S(1)} %get-tuple-elem, ...), custom_call_target="tpu_custom_call" | custom-call | tf_op jit(solution)/shard_map/pallas_call | solution.py:333
  91.2 2.9 %collective-permute-start.11 = (bf16[384,256]{1,0:T(8,128)(2,1)S(1)}, bf16[384,256]{1,0:T(8,128)(2,1)S(1)}, u32[]{:S(2)}, u32[]{:S(2)}) collective-permute-start(bf16[384,256]{1,0:T(8,128)(2,1)S(1)} %get-tuple-element.41), channel_id=1, source_target_pairs={{0,128},{128,256},{256,384},{384,512},{512,640},{640,768},{768,896... | collective-permute-start | bytes 589832 | tf_op jit(solution)/shard_map/ppermute | solution.py:296
  94.1 6.4 %collective-permute-start.12 = (bf16[384,256]{1,0:T(8,128)(2,1)S(1)}, bf16[384,256]{1,0:T(8,128)(2,1)S(1)}, u32[]{:S(2)}, u32[]{:S(2)}) collective-permute-start(bf16[384,256]{1,0:T(8,128)(2,1)S(1)} %get-tuple-element.42), channel_id=1, source_target_pairs={{0,256},{128,384},{256,512},{384,640},{512,768},{640,896},{768,0},... | collective-permute-start | bytes 589832 | tf_op jit(solution)/shard_map/ppermute | solution.py:296
  100.6 1.9 %collective-permute-start.14 = (bf16[384,256]{1,0:T(8,128)(2,1)S(1)}, bf16[384,256]{1,0:T(8,128)(2,1)S(1)}, u32[]{:S(2)}, u32[]{:S(2)}) collective-permute-start(bf16[384,256]{1,0:T(8,128)(2,1)S(1)} %get-tuple-element.44), channel_id=1, source_target_pairs={{0,896},{128,0},{256,128},{384,256},{512,384},{640,512},{768,640},... | collective-permute-start | bytes 589832 | tf_op jit(solution)/shard_map/ppermute | solution.py:296
  102.5 3.9 %collective-permute-start.9 = (bf16[384,256]{1,0:T(8,128)(2,1)}, bf16[384,256]{1,0:T(8,128)(2,1)S(1)}, u32[]{:S(2)}, u32[]{:S(2)}) collective-permute-start(bf16[384,256]{1,0:T(8,128)(2,1)} %get-tuple-element.38), channel_id=1, source_target_pairs={{0,128},{128,256},{256,384},{384,512},{512,640},{640,768},{768,896... | collective-permute-start | bytes 589832 | tf_op jit(solution)/shard_map/ppermute | solution.py:296
  106.5 1.9 %collective-permute-start.10 = (bf16[384,256]{1,0:T(8,128)(2,1)S(1)}, bf16[384,256]{1,0:T(8,128)(2,1)S(1)}, u32[]{:S(2)}, u32[]{:S(2)}) collective-permute-start(bf16[384,256]{1,0:T(8,128)(2,1)S(1)} %get-tuple-element.39), channel_id=1, source_target_pairs={{0,896},{128,0},{256,128},{384,256},{512,384},{640,512},{768,640},... | collective-permute-start | bytes 589832 | tf_op jit(solution)/shard_map/ppermute | solution.py:296
  108.4 4.0 %collective-permute-done.12.s4 = bf16[384,256]{1,0:T(8,128)(2,1)S(1)} collective-permute-done((bf16[384,256]{1,0:T(8,128)(2,1)S(1)}, bf16[384,256]{1,0:T(8,128)(2,1)S(1)}, u32[]{:S(2)}, u32[]{:S(2)}) %collective-permute-start.12) | collective-permute-done | bytes 196640 | tf_op jit(solution)/shard_map/ppermute | solution.py:296
  112.4 2.0 %collective-permute-start.13 = (bf16[384,256]{1,0:T(8,128)(2,1)S(1)}, bf16[384,256]{1,0:T(8,128)(2,1)S(1)}, u32[]{:S(2)}, u32[]{:S(2)}) collective-permute-start(bf16[384,256]{1,0:T(8,128)(2,1)S(1)} %shard_map.127), channel_id=1, source_target_pairs={{0,256},{128,384},{256,512},{384,640},{512,768},{640,896},{768,0},... | collective-permute-start | bytes 589832 | tf_op jit(solution)/shard_map/ppermute | solution.py:296
  114.5 6.0 %collective-permute-start.15 = (bf16[384,256]{1,0:T(8,128)(2,1)S(1)}, bf16[384,256]{1,0:T(8,128)(2,1)S(1)}, u32[]{:S(2)}, u32[]{:S(2)}) collective-permute-start(bf16[384,256]{1,0:T(8,128)(2,1)S(1)} %shard_map.128), channel_id=1, source_target_pairs={{0,768},{128,896},{256,0},{384,128},{512,256},{640,384},{768,512},... | collective-permute-start | bytes 589832 | tf_op jit(solution)/shard_map/ppermute | solution.py:296
  120.5 0.9 shard_map.124
  121.4 2.7 %collective-permute-done.13.t2 = bf16[384,256]{1,0:T(8,128)(2,1)S(1)} collective-permute-done((bf16[384,256]{1,0:T(8,128)(2,1)S(1)}, bf16[384,256]{1,0:T(8,128)(2,1)S(1)}, u32[]{:S(2)}, u32[]{:S(2)}) %collective-permute-start.13) | collective-permute-done | bytes 196640 | tf_op jit(solution)/shard_map/ppermute | solution.py:296
  124.1 3.9 %collective-permute-done.15.t6 = bf16[384,256]{1,0:T(8,128)(2,1)S(1)} collective-permute-done((bf16[384,256]{1,0:T(8,128)(2,1)S(1)}, bf16[384,256]{1,0:T(8,128)(2,1)S(1)}, u32[]{:S(2)}, u32[]{:S(2)}) %collective-permute-start.15) | collective-permute-done | bytes 196640 | tf_op jit(solution)/shard_map/ppermute | solution.py:296
  128.0 0.8 shard_map.129
  (26 shorter events, 1.1 us)
Async XLA Ops:
  3.4 23.6 %copy-start = (bf16[128,256]{1,0:T(8,128)(2,1)S(1)}, bf16[128,256]{1,0:T(8,128)(2,1)}, u32[]{:S(2)}) copy-start(bf16[128,256]{1,0:T(8,128)(2,1)} %w_gate.1) | copy-start | bytes 196612
  3.4 23.6 %copy-start.1 = (bf16[128,256]{1,0:T(8,128)(2,1)S(1)}, bf16[128,256]{1,0:T(8,128)(2,1)}, u32[]{:S(2)}) copy-start(bf16[128,256]{1,0:T(8,128)(2,1)} %w_up.1) | copy-start | bytes 196612
  3.4 23.6 %copy-start.2 = (bf16[256,128]{1,0:T(8,128)(2,1)S(1)}, bf16[256,128]{1,0:T(8,128)(2,1)}, u32[]{:S(2)}) copy-start(bf16[256,128]{1,0:T(8,128)(2,1)} %w_down.1) | copy-start | bytes 196612
  3.4 23.6 %copy-start.4 = (s32[8,2]{0,1:T(2,128)S(1)}, s32[8,2]{0,1:T(2,128)}, u32[]{:S(2)}) copy-start(s32[8,2]{0,1:T(2,128)} %param.9) | copy-start | bytes 196
  3.4 64.9 %all-to-all-start = ((bf16[64,8,1536]{2,1,0:T(8,128)(2,1)}), bf16[64,8,1536]{2,1,0:T(8,128)(2,1)S(1)}, u32[]{:S(2)}, u32[]{:S(2)}) async-start(bf16[64,8,1536]{2,1,0:T(8,128)(2,1)} %shard_map.118), calls=%async_computation | async-start | bytes 3145728 | tf_op jit(solution)/shard_map/all_to_all | solution.py:300
  27.1 13.3 %collective-permute-start.4 = (bf16[392,256]{1,0:T(8,128)(2,1)S(1)}, bf16[392,256]{1,0:T(8,128)(2,1)S(1)}, u32[]{:S(2)}, u32[]{:S(2)}) collective-permute-start(bf16[392,256]{1,0:T(8,128)(2,1)S(1)} %shard_map.120.refs_0_), channel_id=1, source_target_pairs={{0,768},{128,896},{256,0},{384,128},{512,256},{640,384},{768,512},... | collective-permute-start | bytes 602120 | tf_op jit(solution)/shard_map/ppermute | solution.py:296
  31.9 15.9 %collective-permute-start.1 = (bf16[392,256]{1,0:T(8,128)(2,1)S(1)}, bf16[392,256]{1,0:T(8,128)(2,1)S(1)}, u32[]{:S(2)}, u32[]{:S(2)}) collective-permute-start(bf16[392,256]{1,0:T(8,128)(2,1)S(1)} %shard_map.120.refs_0_), channel_id=1, source_target_pairs={{0,256},{128,384},{256,512},{384,640},{512,768},{640,896},{768,0},... | collective-permute-start | bytes 602120 | tf_op jit(solution)/shard_map/ppermute | solution.py:296
  33.9 19.7 %collective-permute-start.6 = (bf16[392,256]{1,0:T(8,128)(2,1)S(1)}, bf16[392,256]{1,0:T(8,128)(2,1)S(1)}, u32[]{:S(2)}, u32[]{:S(2)}) collective-permute-start(bf16[392,256]{1,0:T(8,128)(2,1)S(1)} %shard_map.120.refs_0_), channel_id=1, source_target_pairs={{0,896},{128,0},{256,128},{384,256},{512,384},{640,512},{768,640},... | collective-permute-start | bytes 602120 | tf_op jit(solution)/shard_map/ppermute | solution.py:296
  37.2 16.4 %collective-permute-start = (bf16[392,256]{1,0:T(8,128)(2,1)S(1)}, bf16[392,256]{1,0:T(8,128)(2,1)S(1)}, u32[]{:S(2)}, u32[]{:S(2)}) collective-permute-start(bf16[392,256]{1,0:T(8,128)(2,1)S(1)} %shard_map.120.refs_0_), channel_id=1, source_target_pairs={{0,128},{128,256},{256,384},{384,512},{512,640},{640,768},{768,896... | collective-permute-start | bytes 602120 | tf_op jit(solution)/shard_map/ppermute | solution.py:296
  40.4 13.2 %collective-permute-start.5 = (bf16[392,256]{1,0:T(8,128)(2,1)S(1)}, bf16[392,256]{1,0:T(8,128)(2,1)S(1)}, u32[]{:S(2)}, u32[]{:S(2)}) collective-permute-start(bf16[392,256]{1,0:T(8,128)(2,1)S(1)} %collective-permute-done.4.refs_6_), channel_id=1, source_target_pairs={{0,896},{128,0},{256,128},{384,256},{512,384},{640,512},{768,640},... | collective-permute-start | bytes 602120 | tf_op jit(solution)/shard_map/ppermute | solution.py:296
  47.8 12.4 %collective-permute-start.3 = (bf16[392,256]{1,0:T(8,128)(2,1)S(1)}, bf16[392,256]{1,0:T(8,128)(2,1)S(1)}, u32[]{:S(2)}, u32[]{:S(2)}) collective-permute-start(bf16[392,256]{1,0:T(8,128)(2,1)S(1)} %collective-permute-done.1.refs_2_), channel_id=1, source_target_pairs={{0,256},{128,384},{256,512},{384,640},{512,768},{640,896},{768,0},... | collective-permute-start | bytes 602120 | tf_op jit(solution)/shard_map/ppermute | solution.py:296
  49.7 12.1 %collective-permute-start.2 = (bf16[392,256]{1,0:T(8,128)(2,1)S(1)}, bf16[392,256]{1,0:T(8,128)(2,1)S(1)}, u32[]{:S(2)}, u32[]{:S(2)}) collective-permute-start(bf16[392,256]{1,0:T(8,128)(2,1)S(1)} %collective-permute-done.1.refs_2_), channel_id=1, source_target_pairs={{0,128},{128,256},{256,384},{384,512},{512,640},{640,768},{768,896... | collective-permute-start | bytes 602120 | tf_op jit(solution)/shard_map/ppermute | solution.py:296
  61.9 7.1 %collective-permute-start.7 = (bf16[8,392,256]{2,1,0:T(8,128)(2,1)S(1)}, bf16[8,392,256]{2,1,0:T(8,128)(2,1)}, u32[]{:S(2)}, u32[]{:S(2)}) collective-permute-start(bf16[8,392,256]{2,1,0:T(8,128)(2,1)S(1)} %shard_map.121.own), channel_id=1, source_target_pairs={{0,64},{64,0},{1,65},{65,1},{2,66},{66,2},{3,67},{67,3},{4,68},{68... | collective-permute-start | bytes 4816904 | tf_op jit(solution)/shard_map/ppermute | solution.py:316
  73.3 15.5 %collective-permute-start.8 = (bf16[8,384,256]{2,1,0:T(8,128)(2,1)}, bf16[8,384,256]{2,1,0:T(8,128)(2,1)}, u32[]{:S(2)}, u32[]{:S(2)}) collective-permute-start(bf16[8,384,256]{2,1,0:T(8,128)(2,1)} %get-tuple-element.36), channel_id=1, source_target_pairs={{0,64},{64,0},{1,65},{65,1},{2,66},{66,2},{3,67},{67,3},{4,68},{68... | collective-permute-start | bytes 4718600 | tf_op jit(solution)/shard_map/ppermute | solution.py:330
  77.8 42.7 %all-to-all-start.1 = ((bf16[64,8,896]{2,1,0:T(8,128)(2,1)}), bf16[64,8,896]{2,1,0:T(8,128)(2,1)S(1)}, u32[]{:S(2)}, u32[]{:S(2)}) async-start(bf16[64,8,896]{2,1,0:T(8,128)(2,1)} %bitcast.2), calls=%async_computation.1 | async-start | bytes 1835008 | tf_op jit(solution)/shard_map/all_to_all | solution.py:300
  88.8 31.7 %copy-start.3 = (f32[8,8]{1,0:T(8,128)S(1)}, f32[8,8]{1,0:T(8,128)}, u32[]{:S(2)}) copy-start(f32[8,8]{1,0:T(8,128)} %logits.3) | copy-start | bytes 772
  91.2 17.2 %collective-permute-start.11 = (bf16[384,256]{1,0:T(8,128)(2,1)S(1)}, bf16[384,256]{1,0:T(8,128)(2,1)S(1)}, u32[]{:S(2)}, u32[]{:S(2)}) collective-permute-start(bf16[384,256]{1,0:T(8,128)(2,1)S(1)} %get-tuple-element.41), channel_id=1, source_target_pairs={{0,128},{128,256},{256,384},{384,512},{512,640},{640,768},{768,896... | collective-permute-start | bytes 589832 | tf_op jit(solution)/shard_map/ppermute | solution.py:296
  94.1 18.2 %collective-permute-start.12 = (bf16[384,256]{1,0:T(8,128)(2,1)S(1)}, bf16[384,256]{1,0:T(8,128)(2,1)S(1)}, u32[]{:S(2)}, u32[]{:S(2)}) collective-permute-start(bf16[384,256]{1,0:T(8,128)(2,1)S(1)} %get-tuple-element.42), channel_id=1, source_target_pairs={{0,256},{128,384},{256,512},{384,640},{512,768},{640,896},{768,0},... | collective-permute-start | bytes 589832 | tf_op jit(solution)/shard_map/ppermute | solution.py:296
  100.6 13.8 %collective-permute-start.14 = (bf16[384,256]{1,0:T(8,128)(2,1)S(1)}, bf16[384,256]{1,0:T(8,128)(2,1)S(1)}, u32[]{:S(2)}, u32[]{:S(2)}) collective-permute-start(bf16[384,256]{1,0:T(8,128)(2,1)S(1)} %get-tuple-element.44), channel_id=1, source_target_pairs={{0,896},{128,0},{256,128},{384,256},{512,384},{640,512},{768,640},... | collective-permute-start | bytes 589832 | tf_op jit(solution)/shard_map/ppermute | solution.py:296
  102.5 18.9 %collective-permute-start.9 = (bf16[384,256]{1,0:T(8,128)(2,1)}, bf16[384,256]{1,0:T(8,128)(2,1)S(1)}, u32[]{:S(2)}, u32[]{:S(2)}) collective-permute-start(bf16[384,256]{1,0:T(8,128)(2,1)} %get-tuple-element.38), channel_id=1, source_target_pairs={{0,128},{128,256},{256,384},{384,512},{512,640},{640,768},{768,896... | collective-permute-start | bytes 589832 | tf_op jit(solution)/shard_map/ppermute | solution.py:296
  106.5 15.0 %collective-permute-start.10 = (bf16[384,256]{1,0:T(8,128)(2,1)S(1)}, bf16[384,256]{1,0:T(8,128)(2,1)S(1)}, u32[]{:S(2)}, u32[]{:S(2)}) collective-permute-start(bf16[384,256]{1,0:T(8,128)(2,1)S(1)} %get-tuple-element.39), channel_id=1, source_target_pairs={{0,896},{128,0},{256,128},{384,256},{512,384},{640,512},{768,640},... | collective-permute-start | bytes 589832 | tf_op jit(solution)/shard_map/ppermute | solution.py:296
  112.4 11.7 %collective-permute-start.13 = (bf16[384,256]{1,0:T(8,128)(2,1)S(1)}, bf16[384,256]{1,0:T(8,128)(2,1)S(1)}, u32[]{:S(2)}, u32[]{:S(2)}) collective-permute-start(bf16[384,256]{1,0:T(8,128)(2,1)S(1)} %shard_map.127), channel_id=1, source_target_pairs={{0,256},{128,384},{256,512},{384,640},{512,768},{640,896},{768,0},... | collective-permute-start | bytes 589832 | tf_op jit(solution)/shard_map/ppermute | solution.py:296
  114.5 13.5 %collective-permute-start.15 = (bf16[384,256]{1,0:T(8,128)(2,1)S(1)}, bf16[384,256]{1,0:T(8,128)(2,1)S(1)}, u32[]{:S(2)}, u32[]{:S(2)}) collective-permute-start(bf16[384,256]{1,0:T(8,128)(2,1)S(1)} %shard_map.128), channel_id=1, source_target_pairs={{0,768},{128,896},{256,0},{384,128},{512,256},{640,384},{768,512},... | collective-permute-start | bytes 589832 | tf_op jit(solution)/shard_map/ppermute | solution.py:296
